TPU v7x, 128 devices: a whole 4x4x4 slice. The times are simulated.
128 devices in a mesh: gp: 128 (over z, y, x, core).
Axes of the slice: x: 4, y: 4, z: 4, core: 2. Of those that a mesh axis runs over, the one named last changes fastest.
Arguments:
- features: bfloat16 [1572864, 128], P('gp')
- labels: int32 [1572864], P('gp')
- train_mask: float32 [1572864], P('gp')
- send_idx: int32 [16384, 64], P('gp')
- src_idx: int32 [3145728], P('gp')
- dst_idx: int32 [3145728], P('gp')
- inv_deg: float32 [1572864], P('gp')
- w_self_1: bfloat16 [128, 256], replicated
- w_neigh_1: bfloat16 [128, 256], replicated
- bias_1: float32 [256], replicated
- w_self_2: bfloat16 [256, 256], replicated
- w_neigh_2: bfloat16 [256, 256], replicated
- bias_2: float32 [256], replicated
- w_self_3: bfloat16 [256, 40], replicated
- w_neigh_3: bfloat16 [256, 40], replicated
- bias_3: float32 [40], replicated
Outputs:
- output 1: float32 [], replicated
- output 2: float32 [128, 256], replicated
- output 3: float32 [128, 256], replicated
- output 4: float32 [256], replicated
- output 5: float32 [256, 256], replicated
- output 6: float32 [256, 256], replicated
- output 7: float32 [256], replicated
- output 8: float32 [256, 40], replicated
- output 9: float32 [256, 40], replicated
- output 10: float32 [40], replicated
All inputs are finite; a program needn't handle non-finite values.
Results may differ from a plain program's by a relative error of at most 0.00569115.
Values are sent between devices in bfloat16 or wider.
A program may use at most 1 GiB of HBM per device.

v0:
```python
import jax
import jax.numpy as jnp
from jax import lax
from jax.sharding import PartitionSpec as P

GROUP_AXIS = 'gp'


def aggregate(table, src_idx, dst_idx, inv_deg):
    gathered = jnp.take(table, src_idx, axis=0).astype(jnp.float32)
    summed = jax.ops.segment_sum(gathered, dst_idx, num_segments=inv_deg.shape[0], indices_are_sorted=True)
    return (summed * inv_deg[:, None]).astype(jnp.bfloat16)


def aggregate_grad(d_mean, src_idx, dst_idx, inv_deg, table_rows):
    d_sum = d_mean * inv_deg[:, None]
    return jax.ops.segment_sum(jnp.take(d_sum, dst_idx, axis=0), src_idx, num_segments=table_rows)


def weight_grads(h_in, neigh_mean, d_pre, d_pre_bf):
    g_self = jnp.einsum('nd,ne->de', h_in, d_pre_bf, preferred_element_type=jnp.float32)
    g_neigh = jnp.einsum('nd,ne->de', neigh_mean, d_pre_bf, preferred_element_type=jnp.float32)
    return g_self, g_neigh, jnp.sum(d_pre, axis=0)


def input_grads(d_pre_bf, w_self, w_neigh):
    d_self = jnp.einsum('ne,de->nd', d_pre_bf, w_self, preferred_element_type=jnp.float32)
    d_mean = jnp.einsum('ne,de->nd', d_pre_bf, w_neigh, preferred_element_type=jnp.float32)
    return d_self, d_mean


def head_grad(logits, labels, train_mask):
    log_prob = jax.nn.log_softmax(logits, axis=-1)
    is_label = labels[:, None] == jnp.arange(logits.shape[1], dtype=jnp.int32)[None, :]
    picked = jnp.sum(jnp.where(is_label, log_prob, 0.0), axis=-1)
    d_logits = (jnp.exp(log_prob) - is_label.astype(jnp.float32)) * train_mask[:, None]
    return jnp.sum(train_mask * -picked), d_logits


def solution(mesh):
    def device_step(features, labels, train_mask, send_idx, src_idx, dst_idx, inv_deg,
                    w_self_1, w_neigh_1, bias_1, w_self_2, w_neigh_2, bias_2,
                    w_self_3, w_neigh_3, bias_3):
        n_own = features.shape[0]
        send_flat = send_idx.reshape(-1)
        table_rows = n_own + send_flat.shape[0]

        def layer(hidden, w_self, w_neigh, bias):
            outgoing = jnp.take(hidden, send_flat, axis=0)
            received = lax.all_to_all(outgoing, GROUP_AXIS, 0, 0, tiled=True)
            table = jnp.concatenate([hidden, received], axis=0)
            neigh_mean = aggregate(table, src_idx, dst_idx, inv_deg)
            pre_act = (jnp.dot(hidden, w_self, preferred_element_type=jnp.float32)
                       + jnp.dot(neigh_mean, w_neigh, preferred_element_type=jnp.float32) + bias)
            return neigh_mean, pre_act

        def back_to_owners(d_mean):
            d_table = aggregate_grad(d_mean, src_idx, dst_idx, inv_deg, table_rows)
            returned = lax.all_to_all(d_table[n_own:].astype(jnp.bfloat16), GROUP_AXIS, 0, 0, tiled=True)
            owner_sum = jax.ops.segment_sum(returned.astype(jnp.float32), send_flat, num_segments=n_own)
            return d_table[:n_own] + owner_sum

        mean_1, pre_1 = layer(features, w_self_1, w_neigh_1, bias_1)
        hidden_1 = jax.nn.relu(pre_1).astype(jnp.bfloat16)
        mean_2, pre_2 = layer(hidden_1, w_self_2, w_neigh_2, bias_2)
        hidden_2 = jax.nn.relu(pre_2).astype(jnp.bfloat16)
        mean_3, logits = layer(hidden_2, w_self_3, w_neigh_3, bias_3)
        loss_sum, d_logits = head_grad(logits, labels, train_mask)
        totals = lax.psum(jnp.stack([loss_sum, jnp.sum(train_mask)]), GROUP_AXIS)

        d_pre_3 = d_logits / totals[1]
        d_bf_3 = d_pre_3.astype(jnp.bfloat16)
        g_self_3, g_neigh_3, g_bias_3 = weight_grads(hidden_2, mean_3, d_pre_3, d_bf_3)
        d_self_3, d_mean_3 = input_grads(d_bf_3, w_self_3, w_neigh_3)
        d_pre_2 = jnp.where(pre_2 > 0, d_self_3 + back_to_owners(d_mean_3), 0.0)
        d_bf_2 = d_pre_2.astype(jnp.bfloat16)
        g_self_2, g_neigh_2, g_bias_2 = weight_grads(hidden_1, mean_2, d_pre_2, d_bf_2)
        d_self_2, d_mean_2 = input_grads(d_bf_2, w_self_2, w_neigh_2)
        d_pre_1 = jnp.where(pre_1 > 0, d_self_2 + back_to_owners(d_mean_2), 0.0)
        d_bf_1 = d_pre_1.astype(jnp.bfloat16)
        g_self_1, g_neigh_1, g_bias_1 = weight_grads(features, mean_1, d_pre_1, d_bf_1)

        grads = lax.psum((g_self_1, g_neigh_1, g_bias_1, g_self_2, g_neigh_2, g_bias_2,
                          g_self_3, g_neigh_3, g_bias_3), GROUP_AXIS)
        return (totals[0] / totals[1],) + tuple(grads)

    sharded = P(GROUP_AXIS)
    whole = P()
    return jax.shard_map(device_step, mesh=mesh,
                         in_specs=(sharded,) * 7 + (whole,) * 9,
                         out_specs=(whole,) * 10, check_vma=False)
```

profile of v0, /device:TPU:1, one launch (start us, length us, event | category | flops | bytes accessed | tf_op | source)
XLA Modules:
  0.0 2519.5 jit_solution(6026006220112475705)
XLA Ops:
  9.2 30.5 %gather_fusion = bf16[8192,128]{1,0:T(8,128)(2,1)} fusion(bf16[12288,128]{1,0:T(8,128)(2,1)} %param.22, s32[8192]{0:T(1024)S(1)} %broadcast_clamp_fusion), kind=kCustom, calls=%fused_computation.6 | custom fusion | bytes 4227072 | tf_op jit(solution)/shard_map/jit(_take)/gather | solution.py:49
  39.6 4.6 broadcast_select_fusion.2
  44.2 11.9 all-to-all-start
  56.3 6.3 fusion.54
  62.6 24.2 all-to-all-done
  86.8 12.8 pad_maximum_fusion.2
  99.6 286.9 %scatter_custom_fusion = f32[12288,128]{1,0:T(8,128)} fusion(s32[24576]{0:T(1024)S(1)} %copy-done.7, pred[24576]{0:T(1024)(128)(4,1)S(1)} %compare_and_fusion.1, bf16[]{:T(256)} %constant.63.clone.1, f32[]{:T(128)} %constant.54.clone.1, bf16[20480,128]{1,0:T(8,128)(2,1)} %pad_maximum_fusion.2, s32[24576]{0:T(1024)S(1)} %fusion.39), kind=kCustom, calls=%fused_computation.41 | custom fusion | flops 9437184 | bytes 11657222 | tf_op jit(solution)/shard_map/scatter-add | solution.py:11
  386.6 12.4 maximum_convert_fusion.1
  399.0 34.7 %gather_fusion.1 = bf16[8192,256]{1,0:T(8,128)(2,1)} fusion(bf16[12288,256]{1,0:T(8,128)(2,1)} %get-tuple-element.48, s32[8192]{0:T(1024)S(1)} %fusion.41), kind=kCustom, calls=%fused_computation.clone | custom fusion | bytes 8421376 | tf_op jit(solution)/shard_map/jit(_take)/gather | solution.py:49
  433.7 5.3 broadcast_select_fusion.1
  439.0 6.4 all-to-all-start.1
  445.4 9.1 fusion.55
  454.5 49.7 %all-to-all-done.1 = bf16[128,64,256]{2,1,0:T(8,128)(2,1)} async-done(((bf16[128,64,256]{2,1,0:T(8,128)(2,1)}), bf16[128,64,256]{2,1,0:T(8,128)(2,1)}, u32[]{:S(2)}, u32[]{:S(2)}) %all-to-all-start.1) | async-done | bytes 4194336 | tf_op jit(solution)/shard_map/all_to_all | solution.py:50
  504.2 11.9 pad_maximum_fusion
  516.1 303.9 %scatter_custom_fusion.1 = f32[12288,256]{1,0:T(8,128)} fusion(s32[24576]{0:T(1024)S(1)} %copy-done.7, pred[24576]{0:T(1024)(128)(4,1)S(1)} %compare_and_fusion.1, bf16[]{:T(256)} %constant.63.clone.1, f32[]{:T(128)} %constant.54.clone.1, bf16[20480,256]{1,0:T(8,128)(2,1)} %pad_maximum_fusion, s32[24576]{0:T(1024)S(1)} %fusion.39), kind=kCustom, calls=%fused_computation.21 | custom fusion | flops 18874368 | bytes 23191558 | tf_op jit(solution)/shard_map/scatter-add | solution.py:11
  820.0 16.2 maximum_convert_fusion
  836.2 34.7 %gather_fusion.2 = bf16[8192,256]{1,0:T(8,128)(2,1)} fusion(bf16[12288,256]{1,0:T(8,128)(2,1)} %get-tuple-element.50, s32[8192]{0:T(1024)S(1)} %fusion.41), kind=kCustom, calls=%fused_computation.3.clone | custom fusion | bytes 8421376 | tf_op jit(solution)/shard_map/jit(_take)/gather | solution.py:49
  870.9 5.3 broadcast_select_fusion
  876.2 7.2 all-to-all-start.2
  883.4 6.0 fusion.56
  889.4 52.7 %all-to-all-done.2 = bf16[128,64,256]{2,1,0:T(8,128)(2,1)} async-done(((bf16[128,64,256]{2,1,0:T(8,128)(2,1)}), bf16[128,64,256]{2,1,0:T(8,128)(2,1)}, u32[]{:S(2)}, u32[]{:S(2)}) %all-to-all-start.2) | async-done | bytes 4194336 | tf_op jit(solution)/shard_map/all_to_all | solution.py:50
  942.2 12.0 pad_maximum_fusion.1
  954.2 304.0 %scatter_custom_fusion.2 = f32[12288,256]{1,0:T(8,128)} fusion(s32[24576]{0:T(1024)S(1)} %copy-done.7, pred[24576]{0:T(1024)(128)(4,1)S(1)} %compare_and_fusion.1, bf16[]{:T(256)} %constant.63.clone.1, f32[]{:T(128)} %constant.54.clone.1, bf16[20480,256]{1,0:T(8,128)(2,1)} %pad_maximum_fusion.1, s32[24576]{0:T(1024)S(1)} %fusion.39), kind=kCustom, calls=%fused_computation.19 | custom fusion | flops 18874368 | bytes 23191558 | tf_op jit(solution)/shard_map/scatter-add | solution.py:11
  1258.2 6.3 fusion.53
  1267.4 64.0 %psum.70 = f32[2]{0:T(128)S(1)} all-reduce(f32[2]{0:T(128)S(1)} %pad_maximum_fusion.3), channel_id=1, replica_groups=mesh['gp'=128] {'gp'}, use_global_device_ids=true, to_apply=%region_8.11 | all-reduce | flops 2 | bytes 16 | tf_op jit(solution)/shard_map/psum | solution.py:69
  1334.8 6.5 convolution_multiply_fusion.1
  1341.2 287.9 %scatter_custom_fusion.3 = f32[20480,256]{1,0:T(8,128)} fusion(s32[24576]{0:T(1024)} %param.26, f32[]{:T(128)} %constant.47.clone.2, pred[24576]{0:T(1024)(128)(4,1)S(1)} %compare_and_fusion, f32[]{:T(128)} %constant.54.clone.1, f32[12288,256]{1,0:T(8,128)} %convolution_multiply_fusion.1, s32[24576]{0:T(1024)S(1)} %fusion.40), kind=kCustom, calls=%fused_computation.17 | custom fusion | flops 12582912 | bytes 33678336 | tf_op jit(solution)/shard_map/scatter-add | solution.py:17
  1629.2 5.7 slice.72
  1634.9 5.6 all-to-all-start.3
  1640.5 6.6 fusion.51
  1647.2 10.9 convolution_add_fusion.1
  1658.1 41.1 %all-to-all-done.3 = bf16[128,64,256]{2,1,0:T(8,128)(2,1)} async-done(((bf16[128,64,256]{2,1,0:T(8,128)(2,1)}), bf16[128,64,256]{2,1,0:T(8,128)(2,1)}, u32[]{:S(2)}, u32[]{:S(2)}) %all-to-all-start.3) | async-done | bytes 4194336 | tf_op jit(solution)/shard_map/all_to_all | solution.py:59
  1699.2 54.2 %scatter_custom_fusion.4 = f32[12288,256]{1,0:T(8,128)} fusion(f32[12288,256]{1,0:T(8,128)} %convolution_add_fusion.1, s32[8192]{0:T(1024)} %copy-done.9, bf16[8192,256]{1,0:T(8,128)(2,1)} %bitcast.16), kind=kCustom, calls=%fused_computation.57 | custom fusion | flops 4194304 | bytes 16777216 | tf_op jit(solution)/shard_map/scatter-add | solution.py:60
  1753.4 9.1 fusion.36
  1765.2 5.5 convolution_multiply_fusion
  1770.7 287.5 %scatter_custom_fusion.5 = f32[20480,256]{1,0:T(8,128)} fusion(s32[24576]{0:T(1024)} %param.26, f32[]{:T(128)} %constant.47.clone.2, pred[24576]{0:T(1024)(128)(4,1)S(1)} %compare_and_fusion, f32[]{:T(128)} %constant.54.clone.1, f32[12288,256]{1,0:T(8,128)} %convolution_multiply_fusion, s32[24576]{0:T(1024)S(1)} %fusion.40), kind=kCustom, calls=%fused_computation.15 | custom fusion | flops 12582912 | bytes 33678336 | tf_op jit(solution)/shard_map/scatter-add | solution.py:17
  2058.2 5.7 slice.71
  2064.0 7.0 all-to-all-start.4
  2071.2 4.7 fusion.58
  2075.9 7.3 fusion.57
  2083.2 8.2 fusion.50
  2091.4 11.1 convolution_add_fusion
  2102.5 27.2 %all-to-all-done.4 = bf16[128,64,256]{2,1,0:T(8,128)(2,1)} async-done(((bf16[128,64,256]{2,1,0:T(8,128)(2,1)}), bf16[128,64,256]{2,1,0:T(8,128)(2,1)}, u32[]{:S(2)}, u32[]{:S(2)}) %all-to-all-start.4) | async-done | bytes 4194336 | tf_op jit(solution)/shard_map/all_to_all | solution.py:59
  2129.7 54.4 %scatter_custom_fusion.6 = f32[12288,256]{1,0:T(8,128)} fusion(f32[12288,256]{1,0:T(8,128)} %convolution_add_fusion, s32[8192]{0:T(1024)} %copy-done.9, bf16[8192,256]{1,0:T(8,128)(2,1)} %bitcast.17), kind=kCustom, calls=%fused_computation.55 | custom fusion | flops 4194304 | bytes 16777216 | tf_op jit(solution)/shard_map/scatter-add | solution.py:60
  2184.2 9.3 fusion.34
  2200.0 17.1 fusion.33
  2218.5 129.0 %all-reduce.7.cloned.1.call-done = (f32[128,256]{0,1:T(8,128)}, f32[128,256]{1,0:T(8,128)}, f32[256,256]{1,0:T(8,128)}, f32[256,256]{1,0:T(8,128)}) async-done(((f32[128,256]{0,1:T(8,128)}, f32[128,256]{1,0:T(8,128)}, f32[256,256]{1,0:T(8,128)}, f32[256,256]{1,0:T(8,128)}), (f32[128,256]{0,1:T(8,128)}, f32[128,256]{1,0:T(8,128)}, f32[256,256]{1,0:T(8,128)}, ...) | async-done | bytes 786448 | tf_op jit(solution)/shard_map/psum | solution.py:83
  2349.1 150.7 %all-reduce.5.cloned.1.call-done = (f32[256]{0:T(256)}, f32[256]{0:T(256)}, f32[256,40]{0,1:T(8,128)}, f32[256,40]{0,1:T(8,128)}, f32[40]{0:T(128)}) async-done(((f32[256]{0:T(256)}, f32[256]{0:T(256)}, f32[256,40]{0,1:T(8,128)}, f32[256,40]{0,1:T(8,128)}, f32[40]{0:T(128)}), (f32[256]{0:T(256)}, f32[256]{0:T(256)}, f32[256,40]{0,1:T(8,128)}, f32[256,40]{0,1:T(8,128)}, ...) | async-done | bytes 84144 | tf_op jit(solution)/shard_map/psum | solution.py:83
  (83 shorter events, 30.8 us)
Async XLA Ops:
  7.2 812.8 %copy-start = (bf16[256,256]{1,0:T(8,128)(2,1)S(1)}, bf16[256,256]{1,0:T(8,128)(2,1)}, u32[]{:S(2)}) copy-start(bf16[256,256]{1,0:T(8,128)(2,1)} %param.33) | copy-start | bytes 393220
  39.6 16.6 copy-start.1
  39.6 16.6 copy-start.14
  44.2 42.6 %all-to-all-start = ((bf16[128,64,128]{2,1,0:T(8,128)(2,1)}), bf16[128,64,128]{2,1,0:T(8,128)(2,1)}, u32[]{:S(2)}, u32[]{:S(2)}) async-start(bf16[128,64,128]{2,1,0:T(8,128)(2,1)} %broadcast_select_fusion.2), calls=%async_computation | async-start | bytes 4194304 | tf_op jit(solution)/shard_map/all_to_all | solution.py:50
  56.2 6.3 copy-start.9
  56.3 6.3 copy-start.8
  62.6 37.0 %copy-start.7 = (s32[24576]{0:T(1024)S(1)}, s32[24576]{0:T(1024)}, u32[]{:S(2)}) copy-start(s32[24576]{0:T(1024)} %param.27) | copy-start | bytes 294916
  99.6 286.9 %copy-start.4 = (f32[12288]{0:T(1024)S(1)}, f32[12288]{0:T(1024)}, u32[]{:S(2)}) copy-start(f32[12288]{0:T(1024)} %param.28) | copy-start | bytes 147460
  99.6 286.9 %copy-start.15 = (bf16[128,256]{1,0:T(8,128)(2,1)S(1)}, bf16[128,256]{1,0:T(8,128)(2,1)}, u32[]{:S(2)}) copy-start(bf16[128,256]{1,0:T(8,128)(2,1)} %param.30) | copy-start | bytes 196612
  99.6 286.9 %copy-start.18 = (f32[256]{0:T(256)S(1)}, f32[256]{0:T(256)}, u32[]{:S(2)}) copy-start(f32[256]{0:T(256)} %param.31) | copy-start | bytes 3076
  433.7 11.7 copy-start.5
  439.0 65.2 %all-to-all-start.1 = ((bf16[128,64,256]{2,1,0:T(8,128)(2,1)}), bf16[128,64,256]{2,1,0:T(8,128)(2,1)}, u32[]{:S(2)}, u32[]{:S(2)}) async-start(bf16[128,64,256]{2,1,0:T(8,128)(2,1)} %bitcast.50), calls=%async_computation.1 | async-start | bytes 8388608 | tf_op jit(solution)/shard_map/all_to_all | solution.py:50
  516.1 303.9 %copy-start.16 = (f32[256]{0:T(256)S(1)}, f32[256]{0:T(256)}, u32[]{:S(2)}) copy-start(f32[256]{0:T(256)} %param.34) | copy-start | bytes 3076
  870.8 12.6 copy-start.12
  876.2 66.0 %all-to-all-start.2 = ((bf16[128,64,256]{2,1,0:T(8,128)(2,1)}), bf16[128,64,256]{2,1,0:T(8,128)(2,1)}, u32[]{:S(2)}, u32[]{:S(2)}) async-start(bf16[128,64,256]{2,1,0:T(8,128)(2,1)} %bitcast.49), calls=%async_computation.2 | async-start | bytes 8388608 | tf_op jit(solution)/shard_map/all_to_all | solution.py:50
  954.2 304.0 %copy-start.13 = (bf16[256,40]{0,1:T(8,128)(2,1)S(1)}, bf16[256,40]{0,1:T(8,128)(2,1)}, u32[]{:S(2)}) copy-start(bf16[256,40]{0,1:T(8,128)(2,1)} %param.36) | copy-start | bytes 61444
  954.2 304.0 %copy-start.17 = (f32[40]{0:T(128)S(1)}, f32[40]{0:T(128)}, u32[]{:S(2)}) copy-start(f32[40]{0:T(128)} %param.37) | copy-start | bytes 484
  1258.2 6.7 copy-start.11
  1258.2 7.2 copy-start.10
  1634.9 64.2 %all-to-all-start.3 = ((bf16[128,64,256]{2,1,0:T(8,128)(2,1)}), bf16[128,64,256]{2,1,0:T(8,128)(2,1)}, u32[]{:S(2)}, u32[]{:S(2)}) async-start(bf16[128,64,256]{2,1,0:T(8,128)(2,1)} %bitcast.52), calls=%async_computation.3 | async-start | bytes 8388608 | tf_op jit(solution)/shard_map/all_to_all | solution.py:59
  1762.5 2.7 copy-start.3
  2064.0 65.8 %all-to-all-start.4 = ((bf16[128,64,256]{2,1,0:T(8,128)(2,1)}), bf16[128,64,256]{2,1,0:T(8,128)(2,1)}, u32[]{:S(2)}, u32[]{:S(2)}) async-start(bf16[128,64,256]{2,1,0:T(8,128)(2,1)} %bitcast.51), calls=%async_computation.4 | async-start | bytes 8388608 | tf_op jit(solution)/shard_map/all_to_all | solution.py:59
  2071.0 276.5 %all-reduce.7.cloned.1.call-start = ((), (), s32[]{:S(2)}) async-start(), calls=%async_computation.6 | async-start | bytes 1572864 | tf_op jit(solution)/shard_map/psum | solution.py:83
  2071.2 12.0 slice-start
  2075.9 7.3 slice-start.1
  2083.2 8.2 copy-start.6
  2129.7 63.7 %slice-start.2 = ((s8[6291456]{0:T(1024)(128)(4,1)}), s8[2097152]{0:T(1024)(128)(4,1)S(1)}, s32[]{:S(2)}) async-start(s8[6291456]{0:T(1024)(128)(4,1)} %bitcast.47), calls=%async_computation.9 | async-start | bytes 4194304
  2184.2 9.4 slice-start.3
  2193.6 3.7 copy-start.2
  2200.0 299.8 %all-reduce.5.cloned.1.call-start = ((), (), s32[]{:S(2)}) async-start(), calls=%async_computation.5 | async-start | bytes 168960 | tf_op jit(solution)/shard_map/psum | solution.py:83
Sparse Core Ops, SparseCore 0:
  2200.1 147.3 all-reduce.6
  2354.3 145.3 all-reduce.4
where the time goes:
time: 2540 us; the launch traced here: 2520 us
  other arithmetic  1670 us (66%)
  waiting for transfers between devices  474 us (19%)
  local copies, waits for them, and re-layouts  129 us (5%)
  matrix products  123 us (5%)
  blocking collectives  64 us (3%)
  starting transfers between devices  38.5 us (2%)
    scatter-add x3, other arithmetic, aggregate(): jax.ops.segment_sum(gathered, dst_idx, num_segments=inv_deg.shape[0], ind...  895 us
    scatter-add x2, other arithmetic, aggregate_grad(): jax.ops.segment_sum(jnp.take(d_sum, dst_idx, axis=0), src_idx, num_segmen...  575 us
    psum x2, waiting for transfers between devices, device_step(): lax.psum((g_self_1, g_neigh_1, g_bias_1, g_self_2, g_neigh_2, g_bias_2, g...  280 us
    all_to_all x3, waiting for transfers between devices, layer(): received = lax.all_to_all(outgoing, GROUP_AXIS, 0, 0, tiled=True)  127 us
    scatter-add x2, other arithmetic, back_to_owners(): jax.ops.segment_sum(returned.astype(jnp.float32), send_flat, num_segments...  109 us
    gather x3, local copies, waits for them, and re-layouts, layer(): outgoing = jnp.take(hidden, send_flat, axis=0)  99.8 us
    all_to_all x2, waiting for transfers between devices, back_to_owners(): lax.all_to_all(d_table[n_own:].astype(jnp.bfloat16), GROUP_AXIS, 0, 0, ti...  68.3 us
    psum x1, blocking collectives, device_step(): totals = lax.psum(jnp.stack([loss_sum, jnp.sum(train_mask)]), GROUP_AXIS)  64 us
  transfers between devices with their start and end apart: 7, of which 7 were waited for; matrix products, arithmetic and copies ran while one was open for 4% of the time, Pallas kernels for 0%

commit v1 on v0

v1 whole, which is shorter than its diff:
```python
import math

import jax
import jax.numpy as jnp
from jax import lax
from jax.experimental import pallas as pl
from jax.experimental.pallas import tpu as pltpu
from jax.sharding import PartitionSpec as P

GROUP_AXIS = 'gp'
LANES = 128
SPREAD = 40
BLOCK = 128
TAIL = 8
F32 = jnp.float32
BF16 = jnp.bfloat16
VMEM_LIMIT = 60 * 2 ** 20

SMEM_SPEC = pl.BlockSpec(memory_space=pltpu.SMEM)
HBM_SPEC = pl.BlockSpec(memory_space=pltpu.HBM)


def whole_spec(shape):
    return pl.BlockSpec(shape, lambda i: (0,) * len(shape))


def row_spec(rows, width):
    return pl.BlockSpec((rows, width), lambda i: (i, 0))


def params():
    return pltpu.CompilerParams(vmem_limit_bytes=VMEM_LIMIT, dimension_semantics=('arbitrary',))


def cost(micros):
    return pl.CostEstimate(flops=int(micros * 4e6), bytes_accessed=int(micros * 1e6), transcendentals=0)


def chunk_of(*sizes):
    common = math.gcd(*sizes)
    return max(d for d in range(1, min(common, 1024) + 1) if common % d == 0)


def mm(a, b):
    return jnp.dot(a, b, preferred_element_type=F32)


def tile_linear(row):
    return ((row >> 3) << 4) | (row & 7)


def stream(steps, copies, body):
    for c in copies(0, 0):
        c.start()

    def step(k, carry):
        slot = lax.rem(k, 2)

        @pl.when(k + 1 < steps)
        def _():
            for c in copies(k + 1, 1 - slot):
                c.start()
        for c in copies(k, slot):
            c.wait()
        body(k, slot)
        return carry
    lax.fori_loop(0, steps, step, 0)


def put_rows(tab, row0, x, nc):
    rows = x.shape[0]
    if nc == 1:
        tab[pl.ds(pl.multiple_of(row0, 8), rows), :] = x
    else:
        for g in range(rows // 8):
            for c in range(nc):
                at = pl.multiple_of((row0 + g * 8) * nc + c * 8, 8)
                tab[pl.ds(at, 8), :] = x[g * 8:g * 8 + 8, c * LANES:(c + 1) * LANES]


def load_table(src, tab, row0, stage, sem, nc):
    chunk = stage.shape[1]
    total = src.shape[0]

    def copies(k, slot):
        return [pltpu.make_async_copy(src.at[pl.ds(pl.multiple_of(k * chunk, chunk), chunk), :],
                                      stage.at[slot], sem.at[slot])]

    def body(k, slot):
        step = min(chunk, 128)
        for j in range(chunk // step):
            put_rows(tab, row0 + k * chunk + j * step, stage[slot, j * step:(j + 1) * step, :].astype(F32), nc)
    stream(total // chunk, copies, body)


def zero_rows(acc):
    rows = acc.shape[0]
    step = next(s for s in (256, 128, 64, 32, 16, 8) if rows % s == 0)

    def body(k, carry):
        acc[pl.ds(pl.multiple_of(k * step, step), step), :] = jnp.zeros((step, acc.shape[1]), F32)
        return carry
    lax.fori_loop(0, rows // step, body, 0)


def gather_16(idx, first, tab, nc):
    sub = lax.broadcasted_iota(jnp.int32, (8, LANES), 0)
    halves = [[None, None] for _ in range(nc)]
    for h in range(2):
        for k in range(8):
            at = idx[first + h * 8 + k]
            for c in range(nc):
                row = jnp.broadcast_to(tab[pl.ds(at + 8 * c, 1), :], (8, LANES))
                halves[c][h] = row if k == 0 else jnp.where(sub == k, row, halves[c][h])
    return [jnp.concatenate(halves[c], axis=0).astype(BF16) for c in range(nc)]


def segment_sums(meta, idx, seg, tab, acc, buf, nc, window, blocks):
    first_block, end_block, most = meta[2 * blocks], meta[2 * blocks + 1], meta[2 * blocks + 2]

    def fill(b):
        for g in range(BLOCK // 16):
            parts = gather_16(idx, b * BLOCK + g * 16, tab, nc)
            for c in range(nc):
                buf[g * 16:g * 16 + 16, c * LANES:(c + 1) * LANES] = parts[c]

    def add(b, at):
        at = pl.multiple_of(at, 8)
        rows = lax.broadcasted_iota(jnp.int32, (window, BLOCK), 0) + at
        hot = jnp.where(rows == seg[b], 1.0, 0.0).astype(BF16)
        acc[pl.ds(at, window), :] += mm(hot, buf[...])

    def body(b, carry):
        fill(b)
        add(b, meta[b])
        return carry
    lax.fori_loop(first_block, end_block, body, 0)

    @pl.when(most > 1)
    def _():
        def again(b, carry):
            count = meta[blocks + b]

            @pl.when(count > 1)
            def _():
                fill(b)

                def more(w, c):
                    add(b, meta[b] + w * window)
                    return c
                lax.fori_loop(1, count, more, 0)
            return carry
        lax.fori_loop(first_block, end_block, again, 0)


def spread_lanes():
    return lax.broadcasted_iota(jnp.int32, (1, LANES), 1)


def split3(x):
    hi = x.astype(BF16).astype(F32)
    rest = x - hi
    mid = rest.astype(BF16).astype(F32)
    low = rest - mid
    lane = spread_lanes()
    out = jnp.where(lane < SPREAD, hi, jnp.where(lane < 2 * SPREAD, mid, low))
    return jnp.where(lane < 3 * SPREAD, out, 0.0).astype(BF16)


def fold3(a):
    lane = spread_lanes()
    s = SPREAD
    one = jnp.where(lane < 2 * s, pltpu.roll(a, LANES - s, 1), pltpu.roll(a, 2 * s, 1))
    two = jnp.where(lane < s, pltpu.roll(a, LANES - 2 * s, 1), pltpu.roll(a, s, 1))
    return a + one + two


def add_rows(ref, x):
    ref[...] += jnp.sum(x.reshape(x.shape[0] // 8, 8, x.shape[1]), axis=0)


def pick_rows(name, src, idx, peers, slots, tail):
    n = src.shape[0]
    per = 8
    extra = 0 if tail is None else TAIL
    chunk = chunk_of(n)

    def kern(idx_ref, src_ref, *refs):
        if extra:
            tail_ref, out, tab, stage, sem = refs
        else:
            out, tab, stage, sem = refs

        @pl.when(pl.program_id(0) == 0)
        def _():
            load_table(src_ref, tab, 0, stage, sem, 1)
        first = pl.program_id(0) * (per * slots)

        def body(p, carry):
            for g in range(slots // 16):
                out[p, g * 16:g * 16 + 16, :] = gather_16(idx_ref, first + p * slots + g * 16, tab, 1)[0]
            if extra:
                out[p, slots:slots + extra, :] = tail_ref[...]
            return carry
        lax.fori_loop(0, per, body, 0)

    operands = [idx, src] + ([tail] if extra else [])
    specs = [SMEM_SPEC, HBM_SPEC] + ([whole_spec((TAIL, LANES))] if extra else [])
    return pl.pallas_call(
        kern, name=name, grid=(peers // per,),
        out_shape=jax.ShapeDtypeStruct((peers, slots + extra, LANES), BF16),
        in_specs=specs,
        out_specs=pl.BlockSpec((per, slots + extra, LANES), lambda i: (i, 0, 0)),
        scratch_shapes=[pltpu.VMEM((n, LANES), F32), pltpu.VMEM((2, chunk, LANES), BF16), pltpu.SemaphoreType.DMA((2,))],
        compiler_params=params(), cost_estimate=cost(10))(*operands)


def edge_call(name, edges, nc, table_rows, acc_rows, window, build, hbm_in, blocked, fixed, outs, rows_out, tile,
              epilogue, micros, stage_rows, init=None, extra_scratch=()):
    meta, idx, seg = edges
    blocks = seg.shape[0]
    width = nc * LANES
    steps = rows_out // tile
    nh, nb, nf, no = len(hbm_in), len(blocked), len(fixed), len(outs)
    acc_total = -(-(acc_rows + window) // 256) * 256

    def kern(meta_ref, idx_ref, seg_ref, *refs):
        hb, refs = refs[:nh], refs[nh:]
        bl, refs = refs[:nb], refs[nb:]
        fx, refs = refs[:nf], refs[nf:]
        out, refs = refs[:no], refs[no:]
        tab, acc, buf, stage, sem, isem = refs[:6]
        more = refs[6:]

        @pl.when(pl.program_id(0) == 0)
        def _():
            if init is None:
                zero_rows(acc)
            else:
                start = pltpu.make_async_copy(hb[init], acc.at[pl.ds(0, acc_rows), :], isem)
                start.start()
            build(tab, hb, fx, stage, sem, more)
            if init is not None:
                start.wait()
            segment_sums(meta_ref, idx_ref, seg_ref, tab, acc, buf, nc, window, blocks)
        i = pl.program_id(0)
        at = pl.multiple_of(i * tile, tile)
        epilogue(i, acc[pl.ds(at, tile), :], bl, fx, out)

    out_shape, out_specs = [], []
    for shape, dtype, sums in outs:
        out_shape.append(jax.ShapeDtypeStruct(shape, dtype))
        out_specs.append(whole_spec(shape) if sums else row_spec(tile, shape[1]))
    return pl.pallas_call(
        kern, name=name, grid=(steps,), out_shape=out_shape,
        in_specs=([SMEM_SPEC, SMEM_SPEC, whole_spec(seg.shape)] + [HBM_SPEC] * nh
                  + [row_spec(tile, x.shape[1]) for x in blocked] + [whole_spec(x.shape) for x in fixed]),
        out_specs=out_specs,
        scratch_shapes=[pltpu.VMEM((table_rows * nc, LANES), F32), pltpu.VMEM((acc_total, width), F32),
                        pltpu.VMEM((BLOCK, width), BF16), pltpu.VMEM((2, stage_rows, width), BF16),
                        pltpu.SemaphoreType.DMA((2,)), pltpu.SemaphoreType.DMA(())] + list(extra_scratch),
        compiler_params=params(), cost_estimate=cost(micros))(meta, idx, seg, *hbm_in, *blocked, *fixed)


def edge_meta(seg_first, seg_last, window, first_block, end_block):
    base = seg_first & ~7
    count = (seg_last - base) // window + 1
    tail = jnp.stack([first_block, end_block, jnp.max(count)])
    return jnp.concatenate([base, count, tail]).astype(jnp.int32)


def bits_for(n):
    return max(1, (n - 1).bit_length())


def spread3(w):
    w = jnp.pad(w, ((0, 0), (0, SPREAD - w.shape[1])))
    return jnp.pad(jnp.concatenate([w, w, w], axis=1), ((0, 0), (0, LANES - 3 * SPREAD)))


def lanes_pad(w):
    return jnp.pad(w, ((0, 0), (0, LANES - w.shape[1])))


def solution(mesh):
    peers = mesh.shape[GROUP_AXIS]

    def exchange(x):
        return lax.all_to_all(x, GROUP_AXIS, 0, 0, tiled=True)

    def device_step(features, labels, train_mask, send_idx, src_idx, dst_idx, inv_deg,
                    w_self_1, w_neigh_1, bias_1, w_self_2, w_neigh_2, bias_2,
                    w_self_3, w_neigh_3, bias_3):
        n = features.shape[0]
        slots = send_idx.shape[1]
        halo = peers * slots
        edges = src_idx.shape[0]
        hidden = w_self_1.shape[1]
        classes = w_self_3.shape[1]
        send_flat = send_idx.reshape(-1)
        tile = min(1024, n)
        stage_own = chunk_of(n)
        stage_halo = chunk_of(halo)
        slot_bits = bits_for(halo)
        dst_bits = bits_for(n)
        table = n + halo

        key_src = (src_idx << dst_bits) | dst_idx
        key_send = (send_flat << slot_bits) | jnp.arange(halo, dtype=jnp.int32)
        key_send = jnp.concatenate([key_send, jnp.full((edges - halo,), jnp.iinfo(jnp.int32).max, jnp.int32)])
        ordered = lax.sort(jnp.stack([key_src, key_send]), dimension=1, is_stable=False)
        src_s = ordered[0] >> dst_bits
        dst_s = ordered[0] & ((1 << dst_bits) - 1)
        row_s = ordered[1, :halo] >> slot_bits
        slot_s = ordered[1, :halo] & ((1 << slot_bits) - 1)
        blocks = edges // BLOCK
        halo_blocks = halo // BLOCK
        zero = jnp.int32(0)

        win_f, win_o, win_h, win_r = 128, 176, 176, 240
        far = src_idx - n
        idx_1 = jnp.where(src_idx < n, src_idx, src_idx + TAIL * (far // slots))
        meta_f = edge_meta(dst_idx[::BLOCK], dst_idx[BLOCK - 1::BLOCK], win_f, zero, jnp.int32(blocks))
        seg_f = dst_idx.reshape(blocks, 1, BLOCK)
        fwd_1 = (meta_f, idx_1, seg_f)
        fwd_2 = (meta_f, tile_linear(src_idx), seg_f)
        fwd_3 = (meta_f, src_idx, seg_f)

        owned = jnp.sum((src_idx < n).astype(jnp.int32))
        first, last = src_s[::BLOCK], src_s[BLOCK - 1::BLOCK]
        meta_o = edge_meta(jnp.minimum(first, n - 1), jnp.minimum(last, n - 1), win_o, zero,
                           (owned + BLOCK - 1) // BLOCK)
        meta_h = edge_meta(jnp.maximum(first - n, 0), jnp.maximum(last - n, 0), win_h, owned // BLOCK,
                           jnp.int32(blocks))
        seg_o = src_s.reshape(blocks, 1, BLOCK)
        seg_h = seg_o - n
        meta_r = edge_meta(row_s[::BLOCK], row_s[BLOCK - 1::BLOCK], win_r, zero, jnp.int32(halo_blocks))
        seg_r = row_s.reshape(halo_blocks, 1, BLOCK)
        dst_wide = tile_linear(dst_s)

        inv = jnp.broadcast_to(inv_deg[:, None], (n, LANES))
        b1 = bias_1.reshape(1, -1)
        b2 = bias_2.reshape(1, -1)
        lane = jnp.arange(LANES, dtype=jnp.int32)
        b3 = jnp.where(lane < 3 * SPREAD, spread3(bias_3.reshape(1, -1)), -1e30)
        if classes < SPREAD:
            b3 = jnp.where(lane % SPREAD < classes, b3, -1e30)
        target = jnp.where(lane[None, :] < 3 * SPREAD,
                           train_mask[:, None] * (1.0 + (labels[:, None] == lane[None, :] % SPREAD)), 0.0).astype(BF16)
        ws3, wn3 = spread3(w_self_3), spread3(w_neigh_3)
        ws3_t, wn3_t = lanes_pad(w_self_3).T, lanes_pad(w_neigh_3).T

        marked = jnp.sum(train_mask).astype(jnp.int32)
        digits = jnp.stack([marked // LANES, marked % LANES]).astype(BF16)
        tail = jnp.pad(digits.reshape(1, 2), ((0, TAIL - 1), (0, LANES - 2)))
        out_1 = pick_rows('send_1', features, send_flat, peers, slots, tail)
        got_1 = exchange(out_1)
        counts = got_1[:, slots, :2].astype(F32)
        total = jnp.sum(counts[:, 0]) * LANES + jnp.sum(counts[:, 1])
        got_1_rows = got_1.reshape(peers * (slots + TAIL), LANES)
        rows_1 = got_1_rows.shape[0]

        def own_and_halo(nc, rows_own):
            def build(tab, hb, fx, stage, sem, more):
                load_table(hb[0], tab, 0, stage, sem, nc)
                load_table(hb[1], tab, rows_own, stage, sem, nc)
            return build

        def only(nc):
            def build(tab, hb, fx, stage, sem, more):
                load_table(hb[0], tab, 0, stage, sem, nc)
            return build

        def epi_1(i, a, bl, fx, out):
            mean = (a * bl[1][...]).astype(BF16)
            z = mm(bl[0][...], fx[0][...]) + mm(mean, fx[1][...]) + fx[2][...]
            out[0][...] = mean
            out[1][...] = jnp.maximum(z, 0.0).astype(BF16)

        mean_1, hidden_1 = edge_call(
            'layer_1', fwd_1, 1, n + rows_1, n, win_f, own_and_halo(1, n), [features, got_1_rows],
            [features, inv], [w_self_1, w_neigh_1, b1],
            [((n, LANES), BF16, False), ((n, hidden), BF16, False)], n, tile, epi_1, 40,
            stage_rows=chunk_of(n, rows_1))

        out_2 = pick_rows('send_2', mean_1, send_flat, peers, slots, None)
        got_2 = exchange(out_2)
        group = 8

        def build_2(tab, hb, fx, stage, sem, more):
            load_table(hb[0], tab, 0, stage, sem, 2)
            hb_f, hb_m, sem_m = more

            def copies(k, slot):
                at = pl.ds(k * group, group)
                return [pltpu.make_async_copy(hb[1].at[at], hb_f.at[slot], sem.at[slot]),
                        pltpu.make_async_copy(hb[2].at[at], hb_m.at[slot], sem_m.at[slot])]

            def body(k, slot):
                def one(p, carry):
                    z = (mm(hb_f[slot, p, :slots, :], fx[3][...]) + mm(hb_m[slot, p], fx[4][...]) + fx[5][...])
                    h = jnp.maximum(z, 0.0).astype(BF16).astype(F32)
                    put_rows(tab, n + (k * group + p) * slots, h, 2)
                    return carry
                lax.fori_loop(0, group, one, 0)
            stream(peers // group, copies, body)

        def epi_2(i, a, bl, fx, out):
            scale = bl[1][...]
            mean = (a * jnp.concatenate([scale, scale], axis=1)).astype(BF16)
            z = mm(bl[0][...], fx[0][...]) + mm(mean, fx[1][...]) + fx[2][...]
            h = jnp.maximum(z, 0.0).astype(BF16)
            out[0][...] = mean
            out[1][...] = h
            out[2][...] = split3(mm(h, fx[6][...]))
            out[3][...] = mm(h, fx[7][...])

        mean_2, hidden_2, proj, logits_self = edge_call(
            'layer_2', fwd_2, 2, table, n, win_f, build_2, [hidden_1, got_1, got_2], [hidden_1, inv],
            [w_self_2, w_neigh_2, b2, w_self_1, w_neigh_1, b1, wn3, ws3],
            [((n, hidden), BF16, False), ((n, hidden), BF16, False), ((n, LANES), BF16, False),
             ((n, LANES), F32, False)], n, tile, epi_2, 60, stage_rows=stage_own,
            extra_scratch=[pltpu.VMEM((2, group, slots + TAIL, LANES), BF16), pltpu.VMEM((2, group, slots, LANES), BF16),
                           pltpu.SemaphoreType.DMA((2,))])

        out_3 = pick_rows('send_3', proj, send_flat, peers, slots, None)
        got_3 = exchange(out_3).reshape(halo, LANES)
        inv_total = (1.0 / total).reshape(1, 1)

        def epi_3(i, a, bl, fx, out):
            scale = bl[1][...]
            z = bl[0][...] + fold3(a * scale) + fx[0][...]
            lane = spread_lanes()
            z = jnp.where(lane < 3 * SPREAD, z, -1e30)
            top = jnp.max(z, axis=1, keepdims=True)
            e = jnp.where(lane < SPREAD, jnp.exp(z - top), 0.0)
            lse = top + jnp.log(jnp.sum(e, axis=1, keepdims=True))
            t = bl[2][...].astype(F32)
            hit = t > 1.5
            d = jnp.where(t > 0.5, jnp.exp(z - lse) - jnp.where(hit, 1.0, 0.0), 0.0) * fx[1][...]
            db = d.astype(BF16)
            out[0][...] = db
            out[1][...] = split3(db.astype(F32) * scale)

            @pl.when(i == 0)
            def _():
                out[2][...] = jnp.zeros_like(out[2])
                out[3][...] = jnp.zeros_like(out[3])
            add_rows(out[2], d)
            add_rows(out[3], jnp.where(hit & (lane < SPREAD), lse - z, 0.0))

        d_bf_3, scaled_3, g_b3, loss_parts = edge_call(
            'layer_3', fwd_3, 1, table, n, win_f, own_and_halo(1, n), [proj, got_3],
            [logits_self, inv, target], [b3, jnp.broadcast_to(inv_total, (1, LANES))],
            [((n, LANES), BF16, False), ((n, LANES), BF16, False), ((8, LANES), F32, True), ((8, LANES), F32, True)],
            n, tile, epi_3, 40, stage_rows=chunk_of(n, halo))

        def epi_b3h(i, a, bl, fx, out):
            out[0][...] = split3(fold3(a))

        def epi_plain(i, a, bl, fx, out):
            out[0][...] = a

        tile_h = min(1024, halo)
        back_3 = edge_call('back_3_halo', (meta_h, dst_s, seg_h), 1, n, halo, win_h, only(1), [scaled_3], [], [],
                           [((halo, LANES), BF16, False)], halo, tile_h, epi_b3h, 15, stage_rows=stage_own)[0]
        ret_3 = exchange(back_3.reshape(peers, slots, LANES)).reshape(halo, LANES)
        own_3 = edge_call('back_3_own', (meta_o, dst_s, seg_o), 1, n, n, win_o, only(1), [scaled_3], [], [],
                          [((n, LANES), F32, False)], n, tile, epi_plain, 20, stage_rows=stage_own)[0]

        def epi_o3(i, a, bl, fx, out):
            tb = fold3(a).astype(BF16)
            d_h = mm(bl[0][...], fx[0][...]) + mm(tb, fx[1][...])
            d_pre = jnp.where(bl[1][...] > 0, d_h, 0.0)
            db = d_pre.astype(BF16)
            scale = bl[2][...]
            out[0][...] = tb
            out[1][...] = db
            out[2][...] = (mm(db, fx[2][...]) * jnp.concatenate([scale, scale], axis=1)).astype(BF16)

            @pl.when(i == 0)
            def _():
                out[3][...] = jnp.zeros_like(out[3])
            add_rows(out[3], d_pre)

        tb_3, d_bf_2, scaled_2, g_b2 = edge_call(
            'owner_3', (meta_r, slot_s, seg_r), 1, halo, n, win_r, only(1), [ret_3, own_3],
            [d_bf_3, hidden_2, inv], [ws3_t, wn3_t, w_neigh_2.T],
            [((n, LANES), BF16, False), ((n, hidden), BF16, False), ((n, hidden), BF16, False), ((8, hidden), F32, True)],
            n, tile, epi_o3, 30, init=1, stage_rows=stage_halo)

        def epi_b2h(i, a, bl, fx, out):
            out[0][...] = a.astype(BF16)

        def epi_b2o(i, a, bl, fx, out):
            out[0][...] = a + mm(bl[0][...], fx[0][...])

        back_2 = edge_call('back_2_halo', (meta_h, dst_wide, seg_h), 2, n, halo, win_h, only(2), [scaled_2], [], [],
                           [((halo, hidden), BF16, False)], halo, tile_h, epi_b2h, 20, stage_rows=stage_own)[0]
        ret_2 = exchange(back_2.reshape(peers, slots, hidden)).reshape(halo, hidden)
        own_2 = edge_call('back_2_own', (meta_o, dst_wide, seg_o), 2, n, n, win_o, only(2), [scaled_2], [d_bf_2],
                          [w_self_2.T], [((n, hidden), F32, False)], n, tile, epi_b2o, 30, stage_rows=stage_own)[0]

        def epi_o2(i, a, bl, fx, out):
            d_pre = jnp.where(bl[0][...] > 0, a, 0.0)
            out[0][...] = d_pre.astype(BF16)

            @pl.when(i == 0)
            def _():
                out[1][...] = jnp.zeros_like(out[1])
            add_rows(out[1], d_pre)

        d_bf_1, g_b1 = edge_call(
            'owner_2', (meta_r, tile_linear(slot_s), seg_r), 2, halo, n, win_r, only(2), [ret_2, own_2],
            [hidden_1], [], [((n, hidden), BF16, False), ((8, hidden), F32, True)], n, tile, epi_o2, 25, init=1,
            stage_rows=stage_halo)

        def contract(a, b):
            return jnp.einsum('nd,ne->de', a, b, preferred_element_type=F32)

        parts = [contract(features, d_bf_1), contract(mean_1, d_bf_1), jnp.sum(g_b1, axis=0),
                 contract(hidden_1, d_bf_2), contract(mean_2, d_bf_2), jnp.sum(g_b2, axis=0),
                 contract(hidden_2, d_bf_3)[:, :classes], contract(hidden_2, tb_3)[:, :classes],
                 jnp.sum(g_b3, axis=0)[:classes], jnp.sum(loss_parts).reshape(1)]
        sizes = [p.size for p in parts]
        whole = sum(sizes)
        share = -(-whole // (peers * LANES)) * LANES
        flat = jnp.concatenate([p.reshape(-1) for p in parts] + [jnp.zeros((share * peers - whole,), F32)])
        mine = jnp.sum(exchange(flat.reshape(peers, share)), axis=0)
        full = exchange(jnp.broadcast_to(mine, (peers, share))).reshape(-1)
        outs, at = [], 0
        for p, size in zip(parts, sizes):
            outs.append(full[at:at + size].reshape(p.shape))
            at += size
        return (outs[-1][0] / total,) + tuple(outs[:-1])

    sharded = P(GROUP_AXIS)
    whole = P()
    return jax.shard_map(device_step, mesh=mesh,
                         in_specs=(sharded,) * 7 + (whole,) * 9,
                         out_specs=(whole,) * 10, check_vma=False)
```

time: 2540 us -> 857 us (0.34)
  other arithmetic: 1670 us -> 23.3 us
  Pallas kernels: 0 us -> 540 us
  waiting for transfers between devices: 474 us -> 52.6 us
  matrix products: 123 us -> 27.5 us
  local copies, waits for them, and re-layouts: 129 us -> 97.9 us
    scatter-add x7 -> x0, other arithmetic: 1580 us -> none  [the longest x3 895 us: aggregate(): jax.ops.segment_sum(gathered, dst_idx, num_segments=inv_deg.shape[0], ind...]
    pallas_call x0 -> x12, Pallas kernels: none -> 540 us  [the longest x9 489 us: edge_call(): pl.pallas_call(kern, name=name, grid=(steps,), out_shape=out_shape, in_sp...]
    psum x2 -> x0, waiting for transfers between devices: 280 us -> none  [device_step(): lax.psum((g_self_1, g_neigh_1, g_bias_1, g_self_2, g_neigh_2, g_bias_2, g...]
    all_to_all x5, waiting for transfers between devices: 195 us -> 52.6 us  [exchange(): return lax.all_to_all(x, GROUP_AXIS, 0, 0, tiled=True)]
    dot_general x16 -> x4, matrix products: 123 us -> 17.2 us  [contract(): return jnp.einsum('nd,ne->de', a, b, preferred_element_type=F32)]
    gather x3 -> x0, local copies, waits for them, and re-layouts: 99.8 us -> none  [layer(): outgoing = jnp.take(hidden, send_flat, axis=0)]
    sort x0 -> x2, local copies, waits for them, and re-layouts: none -> 67.9 us  [device_step(): lax.sort(jnp.stack([key_src, key_send]), dimension=1, is_stable=False)]
    psum x1 -> x0, blocking collectives: 64 us -> none  [device_step(): totals = lax.psum(jnp.stack([loss_sum, jnp.sum(train_mask)]), GROUP_AXIS)]
  transfers between devices with their start and end apart: 7 -> 5, of which waited for: 7 -> 2; matrix products, arithmetic and copies ran while one was open for 4% -> 6% of each run, Pallas kernels for 0% -> 10%
where the time goes in v1:
time: 857 us; the launch traced here: 853 us
  Pallas kernels  540 us (63%)
  local copies, waits for them, and re-layouts  97.9 us (11%)
  waiting for transfers between devices  52.6 us (6%)
  blocking collectives  50.7 us (6%)
  starting transfers between devices  39.1 us (5%)
  matrix products  27.5 us (3%)
  other arithmetic  23.3 us (3%)
  between operations  21.8 us (3%)
    pallas_call x9, Pallas kernels, edge_call(): pl.pallas_call(kern, name=name, grid=(steps,), out_shape=out_shape, in_sp...  489 us
    sort x2, local copies, waits for them, and re-layouts, device_step(): lax.sort(jnp.stack([key_src, key_send]), dimension=1, is_stable=False)  67.9 us
    all_to_all x5, waiting for transfers between devices, exchange(): return lax.all_to_all(x, GROUP_AXIS, 0, 0, tiled=True)  52.6 us
    all_to_all x2, blocking collectives, exchange(): return lax.all_to_all(x, GROUP_AXIS, 0, 0, tiled=True)  50.7 us
    pallas_call x3, Pallas kernels, pick_rows(): pl.pallas_call(kern, name=name, grid=(peers // per,), out_shape=jax.Shape...  50.4 us
    all_to_all x5, starting transfers between devices, exchange(): return lax.all_to_all(x, GROUP_AXIS, 0, 0, tiled=True)  39.1 us
    dot_general x4, matrix products, contract(): return jnp.einsum('nd,ne->de', a, b, preferred_element_type=F32)  17.2 us
  transfers between devices with their start and end apart: 5, of which 2 were waited for; matrix products, arithmetic and copies ran while one was open for 6% of the time, Pallas kernels for 10%

profile of v1, /device:TPU:1, one launch (start us, length us, event | category | flops | bytes accessed | tf_op | source)
XLA Modules:
  0.0 852.5 jit_solution(1454918715007560640)
XLA Ops:
  7.2 1.5 reduce_sum.82
  9.4 0.8 copy.76
  11.6 16.8 %send_1.1 = bf16[128,72,128]{2,1,0:T(8,128)(2,1)} custom-call(s32[8192]{0:T(1024)} %reshape.216.idx_ref, bf16[12288,128]{1,0:T(8,128)(2,1)} %refs_2_.1, bf16[8,128]{1,0:T(8,128)(2,1)} %fusion.23.refs_0_), custom_call_target="tpu_custom_call" | custom-call | flops 40000000 | bytes 10000000 | tf_op jit(solution)/shard_map/send_1/pallas_call | solution.py:209
  28.4 11.5 %all-to-all-start = ((bf16[128,72,128]{2,1,0:T(8,128)(2,1)}), bf16[128,72,128]{2,1,0:T(8,128)(2,1)S(1)}, u32[]{:S(2)}, u32[]{:S(2)}) async-start(bf16[128,72,128]{2,1,0:T(8,128)(2,1)} %send_1.1), calls=%async_computation | async-start | bytes 4718592 | tf_op jit(solution)/shard_map/all_to_all | solution.py:289
  40.0 1.4 add_select_fusion
  41.4 0.8 pad_add_fusion
  42.7 67.9 %sort.9.cloned.1.call-done = s32[2,24576]{1,0:T(2,128)} async-done(((s32[2,24576]{1,0:T(2,128)}), s32[2,24576]{1,0:T(2,128)}) %sort.9.cloned.1.call-update) | async-done | bytes 196624 | tf_op jit(solution)/shard_map/sort | solution.py:311
  110.6 1.8 fusion.29
  113.5 1.3 concatenate.38.meta_ref
  114.8 4.1 broadcast_in_dim.40.refs_3_.refs_4_
  118.9 72.1 %layer_1.1 = (bf16[12288,128]{1,0:T(8,128)(2,1)}, bf16[12288,256]{1,0:T(8,128)(2,1)}) custom-call(s32[387]{0:T(512)} %concatenate.38.meta_ref, s32[24576]{0:T(1024)} %get-tuple-element.106.idx_ref, s32[192,1,128]{2,1,0:T(1,128)} %bitcast.76, bf16[12288,128]{1,0:T(8,128)(2,1)} %refs_2_.1, bf16[9216,128]{1,0:T(8,128)(2,1)} %bitcast.66, ...), custom_call_target="tpu_custom_call" | custom-call | flops 160000000 | bytes 40000000 | tf_op jit(solution)/shard_map/layer_1/pallas_call | solution.py:254
  191.0 16.8 %send_2.1 = bf16[128,64,128]{2,1,0:T(8,128)(2,1)} custom-call(s32[8192]{0:T(1024)} %reshape.216.idx_ref, bf16[12288,128]{1,0:T(8,128)(2,1)} %get-tuple-element.27.src_ref), custom_call_target="tpu_custom_call" | custom-call | flops 40000000 | bytes 10000000 | tf_op jit(solution)/shard_map/send_2/pallas_call | solution.py:209
  207.8 9.8 %all-to-all-start.1 = ((bf16[128,64,128]{2,1,0:T(8,128)(2,1)}), bf16[128,64,128]{2,1,0:T(8,128)(2,1)S(1)}, u32[]{:S(2)}, u32[]{:S(2)}) async-start(bf16[128,64,128]{2,1,0:T(8,128)(2,1)} %send_2.1), calls=%async_computation.1 | async-start | bytes 4194304 | tf_op jit(solution)/shard_map/all_to_all | solution.py:289
  221.1 0.8 fusion.15
  221.9 30.0 %all-to-all-done.1.refs_2_ = bf16[128,64,128]{2,1,0:T(8,128)(2,1)S(1)} async-done(((bf16[128,64,128]{2,1,0:T(8,128)(2,1)}), bf16[128,64,128]{2,1,0:T(8,128)(2,1)S(1)}, u32[]{:S(2)}, u32[]{:S(2)}) %all-to-all-start.1) | async-done | bytes 2097184 | tf_op jit(solution)/shard_map/all_to_all | solution.py:289
  251.9 1.3 copy-done.5
  253.2 93.3 %layer_2.1 = (bf16[12288,256]{1,0:T(8,128)(2,1)}, bf16[12288,256]{1,0:T(8,128)(2,1)}, bf16[12288,128]{1,0:T(8,128)(2,1)}, f32[12288,128]{1,0:T(8,128)}) custom-call(s32[387]{0:T(512)} %concatenate.38.meta_ref, s32[24576]{0:T(1024)} %get-tuple-element.107.idx_ref, s32[192,1,128]{2,1,0:T(1,128)} %bitcast.77, ...), custom_call_target="tpu_custom_call" | custom-call | flops 240000000 | bytes 60000000 | tf_op jit(solution)/shard_map/layer_2/pallas_call | solution.py:254
  346.5 16.9 %send_3.1 = bf16[128,64,128]{2,1,0:T(8,128)(2,1)} custom-call(s32[8192]{0:T(1024)} %reshape.216.idx_ref, bf16[12288,128]{1,0:T(8,128)(2,1)} %get-tuple-element.28.src_ref.refs_0_), custom_call_target="tpu_custom_call" | custom-call | flops 40000000 | bytes 10000000 | tf_op jit(solution)/shard_map/send_3/pallas_call | solution.py:209
  363.4 3.9 all-to-all-start.2
  367.3 6.6 select_convert_fusion.refs_4_
  374.0 1.3 concatenate.37.meta_ref
  376.1 1.0 slice_convert_fusion
  379.1 22.6 %all-to-all-done.2 = bf16[128,64,128]{2,1,0:T(8,128)(2,1)S(1)} async-done(((bf16[128,64,128]{2,1,0:T(8,128)(2,1)}), bf16[128,64,128]{2,1,0:T(8,128)(2,1)S(1)}, u32[]{:S(2)}, u32[]{:S(2)}) %all-to-all-start.2) | async-done | bytes 2097184 | tf_op jit(solution)/shard_map/all_to_all | solution.py:289
  402.2 0.8 copy-done.6
  403.0 77.8 %layer_3.1 = (bf16[12288,128]{1,0:T(8,128)(2,1)}, bf16[12288,128]{1,0:T(8,128)(2,1)}, f32[8,128]{1,0:T(8,128)}, f32[8,128]{1,0:T(8,128)}) custom-call(s32[387]{0:T(512)} %concatenate.38.meta_ref, s32[24576]{0:T(1024)} %idx_ref.1, s32[192,1,128]{2,1,0:T(1,128)} %bitcast.78, bf16[12288,128]{1,0:T(8,128)(2,1)} %get-tuple-element.28.src_ref.refs_0_, ...), custom_call_target="tpu_custom_call" | custom-call | flops 160000000 | bytes 40000000 | tf_op jit(solution)/shard_map/layer_3/pallas_call | solution.py:254
  480.9 42.4 %back_3_halo.1 = bf16[8192,128]{1,0:T(8,128)(2,1)} custom-call(s32[387]{0:T(512)} %concatenate.37.meta_ref, s32[24576]{0:T(1024)} %bitcast.79, s32[192,1,128]{2,1,0:T(1,128)} %broadcast_add_fusion.seg_ref, bf16[12288,128]{1,0:T(8,128)(2,1)} %get-tuple-element.30.refs_0_), custom_call_target="tpu_custom_call" | custom-call | flops 60000000 | bytes 15000000 | tf_op jit(solution)/shard_map/back_3_halo/pallas_call | solution.py:254
  523.3 3.8 all-to-all-start.3
  530.2 1.3 concatenate.42.meta_ref
  532.1 1.3 concatenate.36.meta_ref
  534.0 40.0 %back_3_own.1.refs_1_ = f32[12288,128]{1,0:T(8,128)} custom-call(s32[387]{0:T(512)} %concatenate.42.meta_ref, s32[24576]{0:T(1024)} %bitcast.80, s32[192,1,128]{2,1,0:T(1,128)} %get-tuple-element.100.seg_ref, bf16[12288,128]{1,0:T(8,128)(2,1)} %get-tuple-element.30.refs_0_), custom_call_target="tpu_custom_call" | custom-call | flops 80000000 | bytes 20000000 | tf_op jit(solution)/shard_map/back_3_own/pallas_call | solution.py:254
  574.0 1.3 copy-done.4
  575.4 43.0 %owner_3.1 = (bf16[12288,128]{1,0:T(8,128)(2,1)}, bf16[12288,256]{1,0:T(8,128)(2,1)}, bf16[12288,256]{1,0:T(8,128)(2,1)}, f32[8,256]{1,0:T(8,128)}) custom-call(s32[131]{0:T(256)} %concatenate.36.meta_ref, s32[8192]{0:T(1024)} %bitcast.92, s32[64,1,128]{2,1,0:T(1,128)} %get-tuple-element.103.seg_ref, bf16[8192,128]{1,0:T(8,128)(2,1)} %bitcast.68, ...), custom_call_target="tpu_custom_call" | custom-call | flops 120000000 | bytes 30000000 | tf_op jit(solution)/shard_map/owner_3/pallas_call | solution.py:254
  618.4 39.5 %back_2_halo.1 = bf16[8192,256]{1,0:T(8,128)(2,1)} custom-call(s32[387]{0:T(512)} %concatenate.37.meta_ref, s32[24576]{0:T(1024)} %and_or_fusion.1.idx_ref, s32[192,1,128]{2,1,0:T(1,128)} %broadcast_add_fusion.seg_ref, bf16[12288,256]{1,0:T(8,128)(2,1)} %get-tuple-element.33.refs_0_), custom_call_target="tpu_custom_call" | custom-call | flops 80000000 | bytes 20000000 | tf_op jit(solution)/shard_map/back_2_halo/pallas_call | solution.py:254
  657.9 10.2 %all-to-all-start.4 = ((bf16[128,64,256]{2,1,0:T(8,128)(2,1)}), bf16[128,64,256]{2,1,0:T(8,128)(2,1)}, u32[]{:S(2)}, u32[]{:S(2)}) async-start(bf16[128,64,256]{2,1,0:T(8,128)(2,1)} %bitcast.67), calls=%async_computation.4 | async-start | bytes 8388608 | tf_op jit(solution)/shard_map/all_to_all | solution.py:289
  669.6 4.6 fusion.2
  675.0 5.7 fusion
  680.8 6.6 convolution_bitcast_fusion
  687.5 4.6 convolution_bitcast_fusion.1
  692.3 45.9 %back_2_own.1.refs_1_ = f32[12288,256]{1,0:T(8,128)} custom-call(s32[387]{0:T(512)} %concatenate.42.meta_ref, s32[24576]{0:T(1024)} %and_or_fusion.1.idx_ref, s32[192,1,128]{2,1,0:T(1,128)} %get-tuple-element.100.seg_ref, bf16[12288,256]{1,0:T(8,128)(2,1)} %get-tuple-element.33.refs_0_, bf16[12288,256]{1,0:T(8,128)(2,1)} %get-tuple-element.34.refs_1_, ...), custom_call_target="tpu_custom_call" | custom-call | flops 120000000 | bytes 30000000 | tf_op jit(solution)/shard_map/back_2_own/pallas_call | solution.py:254
  738.2 35.3 %owner_2.1 = (bf16[12288,256]{1,0:T(8,128)(2,1)}, f32[8,256]{1,0:T(8,128)}) custom-call(s32[131]{0:T(256)} %concatenate.36.meta_ref, s32[8192]{0:T(1024)} %and_or_fusion.2.idx_ref, s32[64,1,128]{2,1,0:T(1,128)} %get-tuple-element.103.seg_ref, bf16[8192,256]{1,0:T(8,128)(2,1)} %bitcast.29.refs_0_, f32[12288,256]{1,0:T(8,128)} %back_2_own.1.refs_1_, ...), custom_call_target="tpu_custom_call" | custom-call | flops 100000000 | bytes 25000000 | tf_op jit(solution)/shard_map/owner_2/pallas_call | solution.py:254
  773.5 4.1 convolution_bitcast_fusion.2
  778.1 0.9 copy-done.1
  779.0 1.9 convolution_bitcast_fusion.3
  781.3 3.7 concatenate.43
  785.0 28.6 %all_to_all.40 = f32[128,1,1792]{2,1,0:T(1,128)S(1)} all-to-all(f32[128,1,1792]{2,1,0:T(1,128)S(1)} %bitcast.75), channel_id=1, replica_groups=mesh['gp'=128] {'gp'}, dimensions={0} | all-to-all | bytes 1835008 | tf_op jit(solution)/shard_map/all_to_all | solution.py:289
  814.6 22.1 %all_to_all.41 = f32[128,1,1792]{2,1,0:T(1,128)S(1)} all-to-all(f32[128,1,1792]{2,1,0:T(1,128)S(1)} %broadcast_in_dim.46), channel_id=1, replica_groups=mesh['gp'=128] {'gp'}, dimensions={0} | all-to-all | bytes 1835008 | tf_op jit(solution)/shard_map/all_to_all | solution.py:289
  836.7 2.2 reduce.3
  839.1 0.8 fusion.40
  (108 shorter events, 18.1 us)
Async XLA Ops:
  7.2 32.8 %copy-start.13 = (s32[24576]{0:T(1024)S(1)}, s32[24576]{0:T(1024)}, u32[]{:S(2)}) copy-start(s32[24576]{0:T(1024)} %idx_ref.1) | copy-start | bytes 294916
  7.2 32.8 %copy-start.8 = (s32[24576]{0:T(1024)S(1)}, s32[24576]{0:T(1024)}, u32[]{:S(2)}) copy-start(s32[24576]{0:T(1024)} %param.21) | copy-start | bytes 294916
  7.2 107.6 %copy-start.19 = (f32[12288]{0:T(1024)S(1)}, f32[12288]{0:T(1024)}, u32[]{:S(2)}) copy-start(f32[12288]{0:T(1024)} %param.22) | copy-start | bytes 147460
  10.9 29.0 %copy-start.10 = (s32[8192]{0:T(1024)S(1)}, s32[8192]{0:T(1024)}, u32[]{:S(2)}) copy-start(s32[8192]{0:T(1024)} %reshape.216.idx_ref) | copy-start | bytes 98308
  28.4 86.4 %all-to-all-start = ((bf16[128,72,128]{2,1,0:T(8,128)(2,1)}), bf16[128,72,128]{2,1,0:T(8,128)(2,1)S(1)}, u32[]{:S(2)}, u32[]{:S(2)}) async-start(bf16[128,72,128]{2,1,0:T(8,128)(2,1)} %send_1.1), calls=%async_computation | async-start | bytes 4718592 | tf_op jit(solution)/shard_map/all_to_all | solution.py:289
  39.9 70.7 %sort.9.cloned.1.call-start = ((), (), s32[]{:S(2)}) async-start(), calls=%async_computation.7 | async-start | bytes 589856 | tf_op jit(solution)/shard_map/sort | solution.py:311
  114.8 4.1 copy-start.3
  191.0 29.2 %copy-start.17 = (bf16[256,40]{0,1:T(8,128)(2,1)S(1)}, bf16[256,40]{0,1:T(8,128)(2,1)}, u32[]{:S(2)}) copy-start(bf16[256,40]{0,1:T(8,128)(2,1)} %param.30) | copy-start | bytes 61444
  191.0 29.3 %copy-start.18 = (bf16[256,40]{0,1:T(8,128)(2,1)S(1)}, bf16[256,40]{0,1:T(8,128)(2,1)}, u32[]{:S(2)}) copy-start(bf16[256,40]{0,1:T(8,128)(2,1)} %param.29) | copy-start | bytes 61444
  191.0 29.5 %copy-start.25 = (f32[40]{0:T(128)S(1)}, f32[40]{0:T(128)}, u32[]{:S(2)}) copy-start(f32[40]{0:T(128)} %param.31) | copy-start | bytes 484
  207.8 44.0 %all-to-all-start.1 = ((bf16[128,64,128]{2,1,0:T(8,128)(2,1)}), bf16[128,64,128]{2,1,0:T(8,128)(2,1)S(1)}, u32[]{:S(2)}, u32[]{:S(2)}) async-start(bf16[128,64,128]{2,1,0:T(8,128)(2,1)} %send_2.1), calls=%async_computation.1 | async-start | bytes 4194304 | tf_op jit(solution)/shard_map/all_to_all | solution.py:289
  251.9 1.3 copy-start.5
  346.5 20.8 %copy-start.16 = (f32[12288]{0:T(1024)S(1)}, f32[12288]{0:T(1024)}, u32[]{:S(2)}) copy-start(f32[12288]{0:T(1024)} %param.18) | copy-start | bytes 147460
  346.5 20.8 %copy-start.20 = (s32[12288]{0:T(1024)S(1)}, s32[12288]{0:T(1024)}, u32[]{:S(2)}) copy-start(s32[12288]{0:T(1024)} %param.17) | copy-start | bytes 147460
  346.5 28.8 %copy-start.15 = (s32[2,24576]{1,0:T(2,128)S(1)}, s32[2,24576]{1,0:T(2,128)}, u32[]{:S(2)}) copy-start(s32[2,24576]{1,0:T(2,128)} %sort.9.cloned.1.call-done) | copy-start | bytes 589828
  363.4 38.2 %all-to-all-start.2 = ((bf16[128,64,128]{2,1,0:T(8,128)(2,1)}), bf16[128,64,128]{2,1,0:T(8,128)(2,1)S(1)}, u32[]{:S(2)}, u32[]{:S(2)}) async-start(bf16[128,64,128]{2,1,0:T(8,128)(2,1)} %send_3.1), calls=%async_computation.2 | async-start | bytes 4194304 | tf_op jit(solution)/shard_map/all_to_all | solution.py:289
  401.7 1.4 copy-start.6
  480.9 46.9 %copy-start.11 = (bf16[256,256]{1,0:T(8,128)(2,1)S(1)}, bf16[256,256]{1,0:T(8,128)(2,1)}, u32[]{:S(2)}) copy-start(bf16[256,256]{1,0:T(8,128)(2,1)} %refs_6_.1) | copy-start | bytes 393220
  480.9 52.5 %copy-start.9 = (s32[1,24576]{1,0:T(1,128)S(1)}, s32[1,24576]{1,0:T(1,128)}, u32[]{:S(2)}) copy-start(s32[1,24576]{1,0:T(1,128)} %get-tuple-element.101) | copy-start | bytes 294916
  523.3 50.7 %all-to-all-start.3 = ((bf16[128,64,128]{2,1,0:T(8,128)(2,1)}), bf16[128,64,128]{2,1,0:T(8,128)(2,1)S(1)}, u32[]{:S(2)}, u32[]{:S(2)}) async-start(bf16[128,64,128]{2,1,0:T(8,128)(2,1)} %bitcast.69), calls=%async_computation.3 | async-start | bytes 4194304 | tf_op jit(solution)/shard_map/all_to_all | solution.py:289
  574.0 1.4 copy-start.4
  657.9 10.2 %copy-start.12 = (bf16[256,256]{1,0:T(8,128)(2,1)S(1)}, bf16[256,256]{1,0:T(8,128)(2,1)}, u32[]{:S(2)}) copy-start(bf16[256,256]{1,0:T(8,128)(2,1)} %refs_5_.3) | copy-start | bytes 393220
  657.9 11.0 %copy-start.14 = (s32[1,8192]{1,0:T(1,128)S(1)}, s32[1,8192]{1,0:T(1,128)}, u32[]{:S(2)}) copy-start(s32[1,8192]{1,0:T(1,128)} %get-tuple-element.104) | copy-start | bytes 98308
  657.9 11.6 %copy-start.7 = (bf16[12288,128]{1,0:T(8,128)(2,1)S(1)}, bf16[12288,128]{1,0:T(8,128)(2,1)}, u32[]{:S(2)}) copy-start(bf16[12288,128]{1,0:T(8,128)(2,1)} %get-tuple-element.31.refs_2_) | copy-start | bytes 9437188
  657.9 80.2 %all-to-all-start.4 = ((bf16[128,64,256]{2,1,0:T(8,128)(2,1)}), bf16[128,64,256]{2,1,0:T(8,128)(2,1)}, u32[]{:S(2)}, u32[]{:S(2)}) async-start(bf16[128,64,256]{2,1,0:T(8,128)(2,1)} %bitcast.67), calls=%async_computation.4 | async-start | bytes 8388608 | tf_op jit(solution)/shard_map/all_to_all | solution.py:289
  668.2 6.2 copy-start.24
  668.2 6.8 copy-start.23
  675.0 12.6 %slice-start = ((s8[6291456]{0:T(1024)(128)(4,1)}), s8[2097152]{0:T(1024)(128)(4,1)S(1)}, s32[]{:S(2)}) async-start(s8[6291456]{0:T(1024)(128)(4,1)} %bitcast.64), calls=%async_computation.9 | async-start | bytes 4194304
  680.8 6.7 slice-start.1
  687.5 4.8 copy-start.21
  738.2 35.3 %copy-start.2 = (bf16[12288,128]{1,0:T(8,128)(2,1)S(1)}, bf16[12288,128]{1,0:T(8,128)(2,1)}, u32[]{:S(2)}) copy-start(bf16[12288,128]{1,0:T(8,128)(2,1)} %get-tuple-element.27.src_ref) | copy-start | bytes 9437188
  773.5 4.6 copy-start
  773.5 5.5 copy-start.1
  779.0 2.2 copy-start.22
Sparse Core Ops, SparseCore 0:
  43.7 66.8 sort.11.cloned.1.call-done
  (1 shorter events, 0.0 us)

commit v2 on v1

--- a/solution.py
+++ b/solution.py
@@ -11,6 +11,7 @@
 LANES = 128
 SPREAD = 40
 BLOCK = 128
+GROUP = 8
 TAIL = 8
 F32 = jnp.float32
 BF16 = jnp.bfloat16
@@ -36,35 +37,12 @@
     return pl.CostEstimate(flops=int(micros * 4e6), bytes_accessed=int(micros * 1e6), transcendentals=0)
 
 
-def chunk_of(*sizes):
-    common = math.gcd(*sizes)
-    return max(d for d in range(1, min(common, 1024) + 1) if common % d == 0)
-
-
 def mm(a, b):
     return jnp.dot(a, b, preferred_element_type=F32)
 
 
 def tile_linear(row):
     return ((row >> 3) << 4) | (row & 7)
-
-
-def stream(steps, copies, body):
-    for c in copies(0, 0):
-        c.start()
-
-    def step(k, carry):
-        slot = lax.rem(k, 2)
-
-        @pl.when(k + 1 < steps)
-        def _():
-            for c in copies(k + 1, 1 - slot):
-                c.start()
-        for c in copies(k, slot):
-            c.wait()
-        body(k, slot)
-        return carry
-    lax.fori_loop(0, steps, step, 0)
 
 
 def put_rows(tab, row0, x, nc):
@@ -78,19 +56,30 @@
                 tab[pl.ds(at, 8), :] = x[g * 8:g * 8 + 8, c * LANES:(c + 1) * LANES]
 
 
-def load_table(src, tab, row0, stage, sem, nc):
-    chunk = stage.shape[1]
-    total = src.shape[0]
-
-    def copies(k, slot):
-        return [pltpu.make_async_copy(src.at[pl.ds(pl.multiple_of(k * chunk, chunk), chunk), :],
-                                      stage.at[slot], sem.at[slot])]
-
-    def body(k, slot):
-        step = min(chunk, 128)
-        for j in range(chunk // step):
-            put_rows(tab, row0 + k * chunk + j * step, stage[slot, j * step:(j + 1) * step, :].astype(F32), nc)
-    stream(total // chunk, copies, body)
+def fetch(src, stage, sem, parts):
+    rows = src.shape[0] // parts
+    copies = [pltpu.make_async_copy(src.at[pl.ds(k * rows, rows)], stage.at[pl.ds(k * rows, rows)], sem.at[k])
+              for k in range(parts)]
+    for c in copies:
+        c.start()
+    return copies
+
+
+def unpack(copies, stage, tab, row0, nc):
+    rows = stage.shape[0] // len(copies)
+    step = next(d for d in (128, 96, 64, 32, 16) if rows % d == 0)
+    for p, c in enumerate(copies):
+        c.wait()
+
+        def body(k, carry):
+            at = pl.multiple_of(p * rows + k * step, step)
+            put_rows(tab, row0 + at, stage[pl.ds(at, step), :].astype(F32), nc)
+            return carry
+        lax.fori_loop(0, rows // step, body, 0)
+
+
+def group_of(blocks):
+    return next(u for u in (GROUP, 4, 2) if blocks % u == 0)
 
 
 def zero_rows(acc):
@@ -115,26 +104,37 @@
     return [jnp.concatenate(halves[c], axis=0).astype(BF16) for c in range(nc)]
 
 
-def segment_sums(meta, idx, seg, tab, acc, buf, nc, window, blocks):
-    first_block, end_block, most = meta[2 * blocks], meta[2 * blocks + 1], meta[2 * blocks + 2]
-
-    def fill(b):
+def segment_sums(meta, idx, seg, tab, acc, bufs, nc, window, blocks):
+    unroll = group_of(blocks)
+    first_trip, end_trip, most = meta[2 * blocks], meta[2 * blocks + 1], meta[2 * blocks + 2]
+
+    def fill(b, buf):
         for g in range(BLOCK // 16):
             parts = gather_16(idx, b * BLOCK + g * 16, tab, nc)
             for c in range(nc):
                 buf[g * 16:g * 16 + 16, c * LANES:(c + 1) * LANES] = parts[c]
 
-    def add(b, at):
-        at = pl.multiple_of(at, 8)
+    def sums(b, at, buf):
         rows = lax.broadcasted_iota(jnp.int32, (window, BLOCK), 0) + at
-        hot = jnp.where(rows == seg[b], 1.0, 0.0).astype(BF16)
-        acc[pl.ds(at, window), :] += mm(hot, buf[...])
-
-    def body(b, carry):
-        fill(b)
-        add(b, meta[b])
+        return mm(jnp.where(rows == seg[b], 1.0, 0.0).astype(BF16), buf[...])
+
+    def add(at, x):
+        acc[pl.ds(pl.multiple_of(at, 8), window), :] += x
+
+    fill(jnp.minimum(first_trip * unroll, blocks - 1), bufs[0])
+
+    def body(t, carry):
+        before = None
+        for u in range(unroll):
+            b = t * unroll + u
+            now = (meta[b], sums(b, meta[b], bufs[u % 2]))
+            fill(jnp.minimum(b + 1, blocks - 1), bufs[(u + 1) % 2])
+            if before is not None:
+                add(*before)
+            before = now
+        add(*before)
         return carry
-    lax.fori_loop(first_block, end_block, body, 0)
+    lax.fori_loop(first_trip, end_trip, body, 0)
 
     @pl.when(most > 1)
     def _():
@@ -143,14 +143,15 @@
 
             @pl.when(count > 1)
             def _():
-                fill(b)
+                fill(b, bufs[0])
 
                 def more(w, c):
-                    add(b, meta[b] + w * window)
+                    at = meta[b] + w * window
+                    add(at, sums(b, at, bufs[0]))
                     return c
                 lax.fori_loop(1, count, more, 0)
             return carry
-        lax.fori_loop(first_block, end_block, again, 0)
+        lax.fori_loop(first_trip * unroll, end_trip * unroll, again, 0)
 
 
 def spread_lanes():
@@ -181,9 +182,9 @@
 
 def pick_rows(name, src, idx, peers, slots, tail):
     n = src.shape[0]
-    per = 8
+    per = math.gcd(peers, 32)
     extra = 0 if tail is None else TAIL
-    chunk = chunk_of(n)
+    parts = math.gcd(n // 128, 4)
 
     def kern(idx_ref, src_ref, *refs):
         if extra:
@@ -193,7 +194,7 @@
 
         @pl.when(pl.program_id(0) == 0)
         def _():
-            load_table(src_ref, tab, 0, stage, sem, 1)
+            unpack(fetch(src_ref, stage, sem, parts), stage, tab, 0, 1)
         first = pl.program_id(0) * (per * slots)
 
         def body(p, carry):
@@ -211,61 +212,64 @@
         out_shape=jax.ShapeDtypeStruct((peers, slots + extra, LANES), BF16),
         in_specs=specs,
         out_specs=pl.BlockSpec((per, slots + extra, LANES), lambda i: (i, 0, 0)),
-        scratch_shapes=[pltpu.VMEM((n, LANES), F32), pltpu.VMEM((2, chunk, LANES), BF16), pltpu.SemaphoreType.DMA((2,))],
+        scratch_shapes=[pltpu.VMEM((n, LANES), F32), pltpu.VMEM((n, LANES), BF16), pltpu.SemaphoreType.DMA((parts,))],
         compiler_params=params(), cost_estimate=cost(10))(*operands)
 
 
-def edge_call(name, edges, nc, table_rows, acc_rows, window, build, hbm_in, blocked, fixed, outs, rows_out, tile,
-              epilogue, micros, stage_rows, init=None, extra_scratch=()):
+def edge_call(name, edges, nc, table_rows, acc_rows, window, sources, build, hbm_in, blocked, fixed, outs, rows_out,
+              tile, epilogue, micros, init=None):
     meta, idx, seg = edges
     blocks = seg.shape[0]
     width = nc * LANES
-    steps = rows_out // tile
-    nh, nb, nf, no = len(hbm_in), len(blocked), len(fixed), len(outs)
+    nh, nb, nf, no, ns = len(hbm_in), len(blocked), len(fixed), len(outs), len(sources)
     acc_total = -(-(acc_rows + window) // 256) * 256
+    parts = 4
 
     def kern(meta_ref, idx_ref, seg_ref, *refs):
         hb, refs = refs[:nh], refs[nh:]
         bl, refs = refs[:nb], refs[nb:]
         fx, refs = refs[:nf], refs[nf:]
         out, refs = refs[:no], refs[no:]
-        tab, acc, buf, stage, sem, isem = refs[:6]
-        more = refs[6:]
+        tab, acc, buf_0, buf_1, isem = refs[:5]
+        stages, sems = refs[5:5 + ns], refs[5 + ns:]
 
         @pl.when(pl.program_id(0) == 0)
         def _():
+            copies = [fetch(h, st, sm, parts) for h, st, sm in zip(hb, stages, sems)]
             if init is None:
                 zero_rows(acc)
             else:
                 start = pltpu.make_async_copy(hb[init], acc.at[pl.ds(0, acc_rows), :], isem)
                 start.start()
-            build(tab, hb, fx, stage, sem, more)
+            build(copies, stages, tab, fx)
             if init is not None:
                 start.wait()
-            segment_sums(meta_ref, idx_ref, seg_ref, tab, acc, buf, nc, window, blocks)
+            segment_sums(meta_ref, idx_ref, seg_ref, tab, acc, (buf_0, buf_1), nc, window, blocks)
         i = pl.program_id(0)
-        at = pl.multiple_of(i * tile, tile)
-        epilogue(i, acc[pl.ds(at, tile), :], bl, fx, out)
+        epilogue(i, acc[pl.ds(pl.multiple_of(i * tile, tile), tile), :], bl, fx, out)
 
     out_shape, out_specs = [], []
     for shape, dtype, sums in outs:
         out_shape.append(jax.ShapeDtypeStruct(shape, dtype))
         out_specs.append(whole_spec(shape) if sums else row_spec(tile, shape[1]))
     return pl.pallas_call(
-        kern, name=name, grid=(steps,), out_shape=out_shape,
+        kern, name=name, grid=(rows_out // tile,), out_shape=out_shape,
         in_specs=([SMEM_SPEC, SMEM_SPEC, whole_spec(seg.shape)] + [HBM_SPEC] * nh
                   + [row_spec(tile, x.shape[1]) for x in blocked] + [whole_spec(x.shape) for x in fixed]),
         out_specs=out_specs,
-        scratch_shapes=[pltpu.VMEM((table_rows * nc, LANES), F32), pltpu.VMEM((acc_total, width), F32),
-                        pltpu.VMEM((BLOCK, width), BF16), pltpu.VMEM((2, stage_rows, width), BF16),
-                        pltpu.SemaphoreType.DMA((2,)), pltpu.SemaphoreType.DMA(())] + list(extra_scratch),
+        scratch_shapes=([pltpu.VMEM((table_rows * nc, LANES), F32), pltpu.VMEM((acc_total, width), F32),
+                         pltpu.VMEM((BLOCK, width), BF16), pltpu.VMEM((BLOCK, width), BF16),
+                         pltpu.SemaphoreType.DMA(())]
+                        + [pltpu.VMEM(shape, BF16) for shape in sources]
+                        + [pltpu.SemaphoreType.DMA((parts,)) for _ in sources]),
         compiler_params=params(), cost_estimate=cost(micros))(meta, idx, seg, *hbm_in, *blocked, *fixed)
 
 
 def edge_meta(seg_first, seg_last, window, first_block, end_block):
+    unroll = group_of(seg_first.shape[0])
     base = seg_first & ~7
     count = (seg_last - base) // window + 1
-    tail = jnp.stack([first_block, end_block, jnp.max(count)])
+    tail = jnp.stack([first_block // unroll, (end_block + unroll - 1) // unroll, jnp.max(count)])
     return jnp.concatenate([base, count, tail]).astype(jnp.int32)
 
 
@@ -299,25 +303,23 @@
         classes = w_self_3.shape[1]
         send_flat = send_idx.reshape(-1)
         tile = min(1024, n)
-        stage_own = chunk_of(n)
-        stage_halo = chunk_of(halo)
         slot_bits = bits_for(halo)
         dst_bits = bits_for(n)
         table = n + halo
 
         key_src = (src_idx << dst_bits) | dst_idx
         key_send = (send_flat << slot_bits) | jnp.arange(halo, dtype=jnp.int32)
-        key_send = jnp.concatenate([key_send, jnp.full((edges - halo,), jnp.iinfo(jnp.int32).max, jnp.int32)])
-        ordered = lax.sort(jnp.stack([key_src, key_send]), dimension=1, is_stable=False)
-        src_s = ordered[0] >> dst_bits
-        dst_s = ordered[0] & ((1 << dst_bits) - 1)
-        row_s = ordered[1, :halo] >> slot_bits
-        slot_s = ordered[1, :halo] & ((1 << slot_bits) - 1)
+        by_src = lax.sort(key_src, is_stable=False)
+        by_row = lax.sort(key_send, is_stable=False)
+        src_s = by_src >> dst_bits
+        dst_s = by_src & ((1 << dst_bits) - 1)
+        row_s = by_row >> slot_bits
+        slot_s = by_row & ((1 << slot_bits) - 1)
         blocks = edges // BLOCK
         halo_blocks = halo // BLOCK
         zero = jnp.int32(0)
 
-        win_f, win_o, win_h, win_r = 128, 176, 176, 240
+        win_f, win_o, win_h, win_r = 128, 176, 144, 240
         far = src_idx - n
         idx_1 = jnp.where(src_idx < n, src_idx, src_idx + TAIL * (far // slots))
         meta_f = edge_meta(dst_idx[::BLOCK], dst_idx[BLOCK - 1::BLOCK], win_f, zero, jnp.int32(blocks))
@@ -360,15 +362,10 @@
         got_1_rows = got_1.reshape(peers * (slots + TAIL), LANES)
         rows_1 = got_1_rows.shape[0]
 
-        def own_and_halo(nc, rows_own):
-            def build(tab, hb, fx, stage, sem, more):
-                load_table(hb[0], tab, 0, stage, sem, nc)
-                load_table(hb[1], tab, rows_own, stage, sem, nc)
-            return build
-
-        def only(nc):
-            def build(tab, hb, fx, stage, sem, more):
-                load_table(hb[0], tab, 0, stage, sem, nc)
+        def rows_of(nc, *starts):
+            def build(copies, stages, tab, fx):
+                for c, st, row0 in zip(copies, stages, starts):
+                    unpack(c, st, tab, row0, nc)
             return build
 
         def epi_1(i, a, bl, fx, out):
@@ -378,32 +375,30 @@
             out[1][...] = jnp.maximum(z, 0.0).astype(BF16)
 
         mean_1, hidden_1 = edge_call(
-            'layer_1', fwd_1, 1, n + rows_1, n, win_f, own_and_halo(1, n), [features, got_1_rows],
+            'layer_1', fwd_1, 1, n + rows_1, n, win_f, [(n, LANES), (rows_1, LANES)], rows_of(1, 0, n),
+            [features, got_1_rows],
             [features, inv], [w_self_1, w_neigh_1, b1],
-            [((n, LANES), BF16, False), ((n, hidden), BF16, False)], n, tile, epi_1, 40,
-            stage_rows=chunk_of(n, rows_1))
+            [((n, LANES), BF16, False), ((n, hidden), BF16, False)], n, tile, epi_1, 40)
 
         out_2 = pick_rows('send_2', mean_1, send_flat, peers, slots, None)
         got_2 = exchange(out_2)
-        group = 8
-
-        def build_2(tab, hb, fx, stage, sem, more):
-            load_table(hb[0], tab, 0, stage, sem, 2)
-            hb_f, hb_m, sem_m = more
-
-            def copies(k, slot):
-                at = pl.ds(k * group, group)
-                return [pltpu.make_async_copy(hb[1].at[at], hb_f.at[slot], sem.at[slot]),
-                        pltpu.make_async_copy(hb[2].at[at], hb_m.at[slot], sem_m.at[slot])]
-
-            def body(k, slot):
-                def one(p, carry):
-                    z = (mm(hb_f[slot, p, :slots, :], fx[3][...]) + mm(hb_m[slot, p], fx[4][...]) + fx[5][...])
-                    h = jnp.maximum(z, 0.0).astype(BF16).astype(F32)
-                    put_rows(tab, n + (k * group + p) * slots, h, 2)
+
+        def build_2(copies, stages, tab, fx):
+            unpack(copies[0], stages[0], tab, 0, 2)
+            per = peers // len(copies[1])
+            some = math.gcd(per, 8)
+            for p in range(len(copies[1])):
+                copies[1][p].wait()
+                copies[2][p].wait()
+
+                def body(k, carry):
+                    q = p * per + k * some
+                    f = stages[1][pl.ds(q, some), :slots, :].reshape(some * slots, LANES)
+                    m = stages[2][pl.ds(q, some)].reshape(some * slots, LANES)
+                    z = mm(f, fx[3][...]) + mm(m, fx[4][...]) + fx[5][...]
+                    put_rows(tab, n + q * slots, jnp.maximum(z, 0.0).astype(BF16).astype(F32), 2)
                     return carry
-                lax.fori_loop(0, group, one, 0)
-            stream(peers // group, copies, body)
+                lax.fori_loop(0, per // some, body, 0)
 
         def epi_2(i, a, bl, fx, out):
             scale = bl[1][...]
@@ -416,12 +411,11 @@
             out[3][...] = mm(h, fx[7][...])
 
         mean_2, hidden_2, proj, logits_self = edge_call(
-            'layer_2', fwd_2, 2, table, n, win_f, build_2, [hidden_1, got_1, got_2], [hidden_1, inv],
-            [w_self_2, w_neigh_2, b2, w_self_1, w_neigh_1, b1, wn3, ws3],
+            'layer_2', fwd_2, 2, table, n, win_f,
+            [(n, hidden), (peers, slots + TAIL, LANES), (peers, slots, LANES)], build_2, [hidden_1, got_1, got_2],
+            [hidden_1, inv], [w_self_2, w_neigh_2, b2, w_self_1, w_neigh_1, b1, wn3, ws3],
             [((n, hidden), BF16, False), ((n, hidden), BF16, False), ((n, LANES), BF16, False),
-             ((n, LANES), F32, False)], n, tile, epi_2, 60, stage_rows=stage_own,
-            extra_scratch=[pltpu.VMEM((2, group, slots + TAIL, LANES), BF16), pltpu.VMEM((2, group, slots, LANES), BF16),
-                           pltpu.SemaphoreType.DMA((2,))])
+             ((n, LANES), F32, False)], n, tile, epi_2, 60)
 
         out_3 = pick_rows('send_3', proj, send_flat, peers, slots, None)
         got_3 = exchange(out_3).reshape(halo, LANES)
@@ -450,10 +444,10 @@
             add_rows(out[3], jnp.where(hit & (lane < SPREAD), lse - z, 0.0))
 
         d_bf_3, scaled_3, g_b3, loss_parts = edge_call(
-            'layer_3', fwd_3, 1, table, n, win_f, own_and_halo(1, n), [proj, got_3],
+            'layer_3', fwd_3, 1, table, n, win_f, [(n, LANES), (halo, LANES)], rows_of(1, 0, n), [proj, got_3],
             [logits_self, inv, target], [b3, jnp.broadcast_to(inv_total, (1, LANES))],
             [((n, LANES), BF16, False), ((n, LANES), BF16, False), ((8, LANES), F32, True), ((8, LANES), F32, True)],
-            n, tile, epi_3, 40, stage_rows=chunk_of(n, halo))
+            n, tile, epi_3, 40)
 
         def epi_b3h(i, a, bl, fx, out):
             out[0][...] = split3(fold3(a))
@@ -462,11 +456,11 @@
             out[0][...] = a
 
         tile_h = min(1024, halo)
-        back_3 = edge_call('back_3_halo', (meta_h, dst_s, seg_h), 1, n, halo, win_h, only(1), [scaled_3], [], [],
-                           [((halo, LANES), BF16, False)], halo, tile_h, epi_b3h, 15, stage_rows=stage_own)[0]
+        back_3 = edge_call('back_3_halo', (meta_h, dst_s, seg_h), 1, n, halo, win_h, [(n, LANES)], rows_of(1, 0), [scaled_3], [], [],
+                           [((halo, LANES), BF16, False)], halo, tile_h, epi_b3h, 15)[0]
         ret_3 = exchange(back_3.reshape(peers, slots, LANES)).reshape(halo, LANES)
-        own_3 = edge_call('back_3_own', (meta_o, dst_s, seg_o), 1, n, n, win_o, only(1), [scaled_3], [], [],
-                          [((n, LANES), F32, False)], n, tile, epi_plain, 20, stage_rows=stage_own)[0]
+        own_3 = edge_call('back_3_own', (meta_o, dst_s, seg_o), 1, n, n, win_o, [(n, LANES)], rows_of(1, 0), [scaled_3], [], [],
+                          [((n, LANES), F32, False)], n, tile, epi_plain, 20)[0]
 
         def epi_o3(i, a, bl, fx, out):
             tb = fold3(a).astype(BF16)
@@ -484,10 +478,10 @@
             add_rows(out[3], d_pre)
 
         tb_3, d_bf_2, scaled_2, g_b2 = edge_call(
-            'owner_3', (meta_r, slot_s, seg_r), 1, halo, n, win_r, only(1), [ret_3, own_3],
+            'owner_3', (meta_r, slot_s, seg_r), 1, halo, n, win_r, [(halo, LANES)], rows_of(1, 0), [ret_3, own_3],
             [d_bf_3, hidden_2, inv], [ws3_t, wn3_t, w_neigh_2.T],
             [((n, LANES), BF16, False), ((n, hidden), BF16, False), ((n, hidden), BF16, False), ((8, hidden), F32, True)],
-            n, tile, epi_o3, 30, init=1, stage_rows=stage_halo)
+            n, tile, epi_o3, 30, init=1)
 
         def epi_b2h(i, a, bl, fx, out):
             out[0][...] = a.astype(BF16)
@@ -495,11 +489,11 @@
         def epi_b2o(i, a, bl, fx, out):
             out[0][...] = a + mm(bl[0][...], fx[0][...])
 
-        back_2 = edge_call('back_2_halo', (meta_h, dst_wide, seg_h), 2, n, halo, win_h, only(2), [scaled_2], [], [],
-                           [((halo, hidden), BF16, False)], halo, tile_h, epi_b2h, 20, stage_rows=stage_own)[0]
+        back_2 = edge_call('back_2_halo', (meta_h, dst_wide, seg_h), 2, n, halo, win_h, [(n, hidden)], rows_of(2, 0), [scaled_2], [], [],
+                           [((halo, hidden), BF16, False)], halo, tile_h, epi_b2h, 20)[0]
         ret_2 = exchange(back_2.reshape(peers, slots, hidden)).reshape(halo, hidden)
-        own_2 = edge_call('back_2_own', (meta_o, dst_wide, seg_o), 2, n, n, win_o, only(2), [scaled_2], [d_bf_2],
-                          [w_self_2.T], [((n, hidden), F32, False)], n, tile, epi_b2o, 30, stage_rows=stage_own)[0]
+        own_2 = edge_call('back_2_own', (meta_o, dst_wide, seg_o), 2, n, n, win_o, [(n, hidden)], rows_of(2, 0), [scaled_2], [d_bf_2],
+                          [w_self_2.T], [((n, hidden), F32, False)], n, tile, epi_b2o, 30)[0]
 
         def epi_o2(i, a, bl, fx, out):
             d_pre = jnp.where(bl[0][...] > 0, a, 0.0)
@@ -511,9 +505,8 @@
             add_rows(out[1], d_pre)
 
         d_bf_1, g_b1 = edge_call(
-            'owner_2', (meta_r, tile_linear(slot_s), seg_r), 2, halo, n, win_r, only(2), [ret_2, own_2],
-            [hidden_1], [], [((n, hidden), BF16, False), ((8, hidden), F32, True)], n, tile, epi_o2, 25, init=1,
-            stage_rows=stage_halo)
+            'owner_2', (meta_r, tile_linear(slot_s), seg_r), 2, halo, n, win_r, [(halo, hidden)], rows_of(2, 0), [ret_2, own_2],
+            [hidden_1], [], [((n, hidden), BF16, False), ((8, hidden), F32, True)], n, tile, epi_o2, 25, init=1)
 
         def contract(a, b):
             return jnp.einsum('nd,ne->de', a, b, preferred_element_type=F32)

time: 857 us -> 607 us (0.71)
  Pallas kernels: 540 us -> 331 us
  local copies, waits for them, and re-layouts: 97.9 us -> 29.8 us
  waiting for transfers between devices: 52.6 us -> 76 us
  between operations: 21.8 us -> 8.81 us
  other arithmetic: 23.3 us -> 34.2 us
    pallas_call x9, Pallas kernels: 489 us -> 297 us  [edge_call(): pl.pallas_call(kern, name=name, grid=(rows_out // tile,), out_shape=out_s...]
    sort x2 -> x0, local copies, waits for them, and re-layouts: 67.9 us -> none  [device_step(): lax.sort(jnp.stack([key_src, key_send]), dimension=1, is_stable=False)]
    all_to_all x5, waiting for transfers between devices: 52.6 us -> 76 us  [exchange(): return lax.all_to_all(x, GROUP_AXIS, 0, 0, tiled=True)]
    pallas_call x3, Pallas kernels: 50.4 us -> 34.6 us  [pick_rows(): pl.pallas_call(kern, name=name, grid=(peers // per,), out_shape=jax.Shape...]
    sort x0 -> x2, other arithmetic: none -> 14.2 us  [the longest x1 8.59 us: device_step(): by_src = lax.sort(key_src, is_stable=False)]
  transfers between devices with their start and end apart: 5 -> 5, of which waited for: 2 -> 4; matrix products, arithmetic and copies ran while one was open for 6% -> 10% of each run, Pallas kernels for 10% -> 9%
where the time goes in v2:
time: 607 us; the launch traced here: 597 us
  Pallas kernels  331 us (55%)
  waiting for transfers between devices  76 us (13%)
  blocking collectives  48.1 us (8%)
  starting transfers between devices  41.6 us (7%)
  other arithmetic  34.2 us (6%)
  local copies, waits for them, and re-layouts  29.8 us (5%)
  matrix products  27.5 us (5%)
  between operations  8.81 us (1%)
    pallas_call x9, Pallas kernels, edge_call(): pl.pallas_call(kern, name=name, grid=(rows_out // tile,), out_shape=out_s...  297 us
    all_to_all x5, waiting for transfers between devices, exchange(): return lax.all_to_all(x, GROUP_AXIS, 0, 0, tiled=True)  76 us
    all_to_all x2, blocking collectives, exchange(): return lax.all_to_all(x, GROUP_AXIS, 0, 0, tiled=True)  48.1 us
    all_to_all x5, starting transfers between devices, exchange(): return lax.all_to_all(x, GROUP_AXIS, 0, 0, tiled=True)  41.6 us
    pallas_call x3, Pallas kernels, pick_rows(): pl.pallas_call(kern, name=name, grid=(peers // per,), out_shape=jax.Shape...  34.6 us
    dot_general x4, matrix products, contract(): return jnp.einsum('nd,ne->de', a, b, preferred_element_type=F32)  17.2 us
  transfers between devices with their start and end apart: 5, of which 4 were waited for; matrix products, arithmetic and copies ran while one was open for 10% of the time, Pallas kernels for 9%

profile of v2, /device:TPU:1, one launch (start us, length us, event | category | flops | bytes accessed | tf_op | source)
XLA Modules:
  0.0 597.3 jit_solution(366990739643010723)
XLA Ops:
  0.7 1.5 reduce_sum.82
  2.8 0.8 copy.76
  5.0 11.5 %send_1.1 = bf16[128,72,128]{2,1,0:T(8,128)(2,1)} custom-call(s32[8192]{0:T(1024)} %reshape.190.idx_ref, bf16[12288,128]{1,0:T(8,128)(2,1)} %refs_2_.1, bf16[8,128]{1,0:T(8,128)(2,1)} %fusion.23.refs_0_), custom_call_target="tpu_custom_call" | custom-call | flops 40000000 | bytes 10000000 | tf_op jit(solution)/shard_map/send_1/pallas_call | solution.py:210
  16.6 11.5 %all-to-all-start = ((bf16[128,72,128]{2,1,0:T(8,128)(2,1)}), bf16[128,72,128]{2,1,0:T(8,128)(2,1)S(1)}, u32[]{:S(2)}, u32[]{:S(2)}) async-start(bf16[128,72,128]{2,1,0:T(8,128)(2,1)} %send_1.1), calls=%async_computation | async-start | bytes 4718592 | tf_op jit(solution)/shard_map/all_to_all | solution.py:293
  28.1 1.4 add_select_fusion
  29.5 8.6 %sort.15 = s32[24576]{0:T(1024)S(1)} sort(s32[24576]{0:T(1024)S(1)} %get-tuple-element.103), dimensions={0}, to_apply=%region_2.3 | sort | flops 368640 | bytes 196608 | tf_op jit(solution)/shard_map/sort | solution.py:312
  40.4 1.3 concatenate.34.meta_ref
  41.7 22.1 %all-to-all-done.refs_1_ = bf16[128,72,128]{2,1,0:T(8,128)(2,1)S(1)} async-done(((bf16[128,72,128]{2,1,0:T(8,128)(2,1)}), bf16[128,72,128]{2,1,0:T(8,128)(2,1)S(1)}, u32[]{:S(2)}, u32[]{:S(2)}) %all-to-all-start) | async-done | bytes 2359328 | tf_op jit(solution)/shard_map/all_to_all | solution.py:293
  63.8 4.1 broadcast_in_dim.39.refs_3_.refs_4_
  67.9 40.8 %layer_1.1 = (bf16[12288,128]{1,0:T(8,128)(2,1)}, bf16[12288,256]{1,0:T(8,128)(2,1)}) custom-call(s32[387]{0:T(512)} %concatenate.34.meta_ref, s32[24576]{0:T(1024)} %get-tuple-element.100.idx_ref, s32[192,1,128]{2,1,0:T(1,128)} %bitcast.67, bf16[12288,128]{1,0:T(8,128)(2,1)} %refs_2_.1, bf16[9216,128]{1,0:T(8,128)(2,1)} %bitcast.57, ...), custom_call_target="tpu_custom_call" | custom-call | flops 160000000 | bytes 40000000 | tf_op jit(solution)/shard_map/layer_1/pallas_call | solution.py:255
  108.7 11.5 %send_2.1 = bf16[128,64,128]{2,1,0:T(8,128)(2,1)} custom-call(s32[8192]{0:T(1024)} %reshape.190.idx_ref, bf16[12288,128]{1,0:T(8,128)(2,1)} %get-tuple-element.27.src_ref), custom_call_target="tpu_custom_call" | custom-call | flops 40000000 | bytes 10000000 | tf_op jit(solution)/shard_map/send_2/pallas_call | solution.py:210
  120.3 5.1 all-to-all-start.1
  128.2 1.3 concatenate.33.meta_ref
  131.6 24.6 %all-to-all-done.1.refs_2_ = bf16[128,64,128]{2,1,0:T(8,128)(2,1)S(1)} async-done(((bf16[128,64,128]{2,1,0:T(8,128)(2,1)}), bf16[128,64,128]{2,1,0:T(8,128)(2,1)S(1)}, u32[]{:S(2)}, u32[]{:S(2)}) %all-to-all-start.1) | async-done | bytes 2097184 | tf_op jit(solution)/shard_map/all_to_all | solution.py:293
  156.2 1.3 copy-done.5
  157.5 52.4 %layer_2.1 = (bf16[12288,256]{1,0:T(8,128)(2,1)}, bf16[12288,256]{1,0:T(8,128)(2,1)}, bf16[12288,128]{1,0:T(8,128)(2,1)}, f32[12288,128]{1,0:T(8,128)}) custom-call(s32[387]{0:T(512)} %concatenate.34.meta_ref, s32[24576]{0:T(1024)} %get-tuple-element.101.idx_ref, s32[192,1,128]{2,1,0:T(1,128)} %bitcast.68, ...), custom_call_target="tpu_custom_call" | custom-call | flops 240000000 | bytes 60000000 | tf_op jit(solution)/shard_map/layer_2/pallas_call | solution.py:255
  210.0 11.6 %send_3.1 = bf16[128,64,128]{2,1,0:T(8,128)(2,1)} custom-call(s32[8192]{0:T(1024)} %reshape.190.idx_ref, bf16[12288,128]{1,0:T(8,128)(2,1)} %get-tuple-element.28.src_ref.refs_0_), custom_call_target="tpu_custom_call" | custom-call | flops 40000000 | bytes 10000000 | tf_op jit(solution)/shard_map/send_3/pallas_call | solution.py:210
  221.5 5.7 all-to-all-start.2
  227.2 6.6 %select_convert_fusion.refs_4_ = bf16[12288,128]{1,0:T(8,128)(2,1)} fusion(s32[128]{0:T(128)S(1)} %and_select_fusion.1, f32[12288]{0:T(1024)S(1)} %copy-done.15, s32[12288]{0:T(1024)S(1)} %copy-done.19, pred[128]{0:T(512)(128)(4,1)S(1)} %iota_compare_fusion.3), kind=kLoop, calls=%fused_computation | loop fusion | flops 9437184 | bytes 3244672 | tf_op jit(solution)/shard_map/convert_element_type | solution.py:351
  233.9 1.0 slice_convert_fusion
  236.9 24.7 %all-to-all-done.2 = bf16[128,64,128]{2,1,0:T(8,128)(2,1)S(1)} async-done(((bf16[128,64,128]{2,1,0:T(8,128)(2,1)}), bf16[128,64,128]{2,1,0:T(8,128)(2,1)S(1)}, u32[]{:S(2)}, u32[]{:S(2)}) %all-to-all-start.2) | async-done | bytes 2097184 | tf_op jit(solution)/shard_map/all_to_all | solution.py:293
  262.1 0.8 copy-done.6
  262.9 47.4 %layer_3.1 = (bf16[12288,128]{1,0:T(8,128)(2,1)}, bf16[12288,128]{1,0:T(8,128)(2,1)}, f32[8,128]{1,0:T(8,128)}, f32[8,128]{1,0:T(8,128)}) custom-call(s32[387]{0:T(512)} %concatenate.34.meta_ref, s32[24576]{0:T(1024)} %idx_ref.1, s32[192,1,128]{2,1,0:T(1,128)} %bitcast.69, bf16[12288,128]{1,0:T(8,128)(2,1)} %get-tuple-element.28.src_ref.refs_0_, ...), custom_call_target="tpu_custom_call" | custom-call | flops 160000000 | bytes 40000000 | tf_op jit(solution)/shard_map/layer_3/pallas_call | solution.py:255
  310.4 23.5 %back_3_halo.1 = bf16[8192,128]{1,0:T(8,128)(2,1)} custom-call(s32[387]{0:T(512)} %concatenate.33.meta_ref, s32[24576]{0:T(1024)} %get-tuple-element.104.idx_ref, s32[192,1,128]{2,1,0:T(1,128)} %broadcast_add_fusion.seg_ref, bf16[12288,128]{1,0:T(8,128)(2,1)} %get-tuple-element.30.refs_0_), custom_call_target="tpu_custom_call" | custom-call | flops 60000000 | bytes 15000000 | tf_op jit(solution)/shard_map/back_3_halo/pallas_call | solution.py:255
  333.8 6.1 %all-to-all-start.3 = ((bf16[128,64,128]{2,1,0:T(8,128)(2,1)}), bf16[128,64,128]{2,1,0:T(8,128)(2,1)S(1)}, u32[]{:S(2)}, u32[]{:S(2)}) async-start(bf16[128,64,128]{2,1,0:T(8,128)(2,1)} %bitcast.60), calls=%async_computation.3 | async-start | bytes 4194304 | tf_op jit(solution)/shard_map/all_to_all | solution.py:293
  340.6 5.6 sort.14
  347.9 1.3 concatenate.38.meta_ref
  349.8 1.3 concatenate.32.meta_ref
  351.8 23.3 %back_3_own.1.refs_1_ = f32[12288,128]{1,0:T(8,128)} custom-call(s32[387]{0:T(512)} %concatenate.38.meta_ref, s32[24576]{0:T(1024)} %get-tuple-element.104.idx_ref, s32[192,1,128]{2,1,0:T(1,128)} %bitcast.71, bf16[12288,128]{1,0:T(8,128)(2,1)} %get-tuple-element.30.refs_0_), custom_call_target="tpu_custom_call" | custom-call | flops 80000000 | bytes 20000000 | tf_op jit(solution)/shard_map/back_3_own/pallas_call | solution.py:255
  375.1 1.3 copy-done.4
  376.4 31.5 %owner_3.1 = (bf16[12288,128]{1,0:T(8,128)(2,1)}, bf16[12288,256]{1,0:T(8,128)(2,1)}, bf16[12288,256]{1,0:T(8,128)(2,1)}, f32[8,256]{1,0:T(8,128)}) custom-call(s32[131]{0:T(256)} %concatenate.32.meta_ref, s32[8192]{0:T(1024)} %get-tuple-element.107.idx_ref, s32[64,1,128]{2,1,0:T(1,128)} %bitcast.81, bf16[8192,128]{1,0:T(8,128)(2,1)} %bitcast.59, ...), custom_call_target="tpu_custom_call" | custom-call | flops 120000000 | bytes 30000000 | tf_op jit(solution)/shard_map/owner_3/pallas_call | solution.py:255
  407.9 21.7 %back_2_halo.1 = bf16[8192,256]{1,0:T(8,128)(2,1)} custom-call(s32[387]{0:T(512)} %concatenate.33.meta_ref, s32[24576]{0:T(1024)} %get-tuple-element.105.idx_ref, s32[192,1,128]{2,1,0:T(1,128)} %broadcast_add_fusion.seg_ref, bf16[12288,256]{1,0:T(8,128)(2,1)} %get-tuple-element.33.refs_0_), custom_call_target="tpu_custom_call" | custom-call | flops 80000000 | bytes 20000000 | tf_op jit(solution)/shard_map/back_2_halo/pallas_call | solution.py:255
  429.6 13.3 %all-to-all-start.4 = ((bf16[128,64,256]{2,1,0:T(8,128)(2,1)}), bf16[128,64,256]{2,1,0:T(8,128)(2,1)}, u32[]{:S(2)}, u32[]{:S(2)}) async-start(bf16[128,64,256]{2,1,0:T(8,128)(2,1)} %bitcast.58), calls=%async_computation.4 | async-start | bytes 8388608 | tf_op jit(solution)/shard_map/all_to_all | solution.py:293
  443.7 4.6 fusion.2
  449.1 5.7 fusion
  454.9 6.6 %convolution_bitcast_fusion = f32[32,2,8,128]{3,2,1,0:T(8,128)S(1)} fusion(bf16[12288,256]{1,0:T(8,128)(2,1)} %get-tuple-element.37, bf16[12288,256]{1,0:T(8,128)(2,1)} %get-tuple-element.34.refs_1_), kind=kOutput, calls=%fused_computation.5 | convolution fusion | flops 1610612736 | bytes 12845056 | tf_op jit(solution)/shard_map/nd,ne->de/dot_general | solution.py:512
  461.7 4.6 convolution_bitcast_fusion.1
  466.5 30.3 %back_2_own.1.refs_1_ = f32[12288,256]{1,0:T(8,128)} custom-call(s32[387]{0:T(512)} %concatenate.38.meta_ref, s32[24576]{0:T(1024)} %get-tuple-element.105.idx_ref, s32[192,1,128]{2,1,0:T(1,128)} %bitcast.72, bf16[12288,256]{1,0:T(8,128)(2,1)} %get-tuple-element.33.refs_0_, bf16[12288,256]{1,0:T(8,128)(2,1)} %get-tuple-element.34.refs_1_, ...), custom_call_target="tpu_custom_call" | custom-call | flops 120000000 | bytes 30000000 | tf_op jit(solution)/shard_map/back_2_own/pallas_call | solution.py:255
  496.8 4.6 all-to-all-done.4
  501.5 25.7 %owner_2.1 = (bf16[12288,256]{1,0:T(8,128)(2,1)}, f32[8,256]{1,0:T(8,128)}) custom-call(s32[131]{0:T(256)} %concatenate.32.meta_ref, s32[8192]{0:T(1024)} %get-tuple-element.108.idx_ref, s32[64,1,128]{2,1,0:T(1,128)} %bitcast.82, bf16[8192,256]{1,0:T(8,128)(2,1)} %bitcast.23.refs_0_, f32[12288,256]{1,0:T(8,128)} %back_2_own.1.refs_1_, ...), custom_call_target="tpu_custom_call" | custom-call | flops 100000000 | bytes 25000000 | tf_op jit(solution)/shard_map/owner_2/pallas_call | solution.py:255
  527.2 4.1 convolution_bitcast_fusion.2
  531.8 0.9 copy-done.1
  532.7 1.9 convolution_bitcast_fusion.3
  535.0 3.7 concatenate.39
  538.7 26.0 %all_to_all.40 = f32[128,1,1792]{2,1,0:T(1,128)S(1)} all-to-all(f32[128,1,1792]{2,1,0:T(1,128)S(1)} %bitcast.66), channel_id=1, replica_groups=mesh['gp'=128] {'gp'}, dimensions={0} | all-to-all | bytes 1835008 | tf_op jit(solution)/shard_map/all_to_all | solution.py:293
  565.8 22.1 %all_to_all.41 = f32[128,1,1792]{2,1,0:T(1,128)S(1)} all-to-all(f32[128,1,1792]{2,1,0:T(1,128)S(1)} %broadcast_in_dim.45), channel_id=1, replica_groups=mesh['gp'=128] {'gp'}, dimensions={0} | all-to-all | bytes 1835008 | tf_op jit(solution)/shard_map/all_to_all | solution.py:293
  587.9 2.2 reduce.3
  590.2 0.8 fusion.38
  (101 shorter events, 18.1 us)
Async XLA Ops:
  0.6 27.4 %copy-start.13 = (s32[24576]{0:T(1024)S(1)}, s32[24576]{0:T(1024)}, u32[]{:S(2)}) copy-start(s32[24576]{0:T(1024)} %idx_ref.1) | copy-start | bytes 294916
  0.7 27.4 %copy-start.8 = (s32[24576]{0:T(1024)S(1)}, s32[24576]{0:T(1024)}, u32[]{:S(2)}) copy-start(s32[24576]{0:T(1024)} %param.21) | copy-start | bytes 294916
  0.7 63.1 %copy-start.18 = (f32[12288]{0:T(1024)S(1)}, f32[12288]{0:T(1024)}, u32[]{:S(2)}) copy-start(f32[12288]{0:T(1024)} %param.22) | copy-start | bytes 147460
  16.6 47.2 %all-to-all-start = ((bf16[128,72,128]{2,1,0:T(8,128)(2,1)}), bf16[128,72,128]{2,1,0:T(8,128)(2,1)S(1)}, u32[]{:S(2)}, u32[]{:S(2)}) async-start(bf16[128,72,128]{2,1,0:T(8,128)(2,1)} %send_1.1), calls=%async_computation | async-start | bytes 4718592 | tf_op jit(solution)/shard_map/all_to_all | solution.py:293
  38.8 92.1 %copy-start.9 = (s32[24576]{0:T(1024)}, s32[24576]{0:T(1024)S(1)}, u32[]{:S(2)}) copy-start(s32[24576]{0:T(1024)S(1)} %get-tuple-element.106) | copy-start | bytes 294916
  63.8 4.1 copy-start.3
  108.7 19.3 %copy-start.16 = (bf16[256,40]{0,1:T(8,128)(2,1)S(1)}, bf16[256,40]{0,1:T(8,128)(2,1)}, u32[]{:S(2)}) copy-start(bf16[256,40]{0,1:T(8,128)(2,1)} %param.30) | copy-start | bytes 61444
  108.7 19.4 %copy-start.17 = (bf16[256,40]{0,1:T(8,128)(2,1)S(1)}, bf16[256,40]{0,1:T(8,128)(2,1)}, u32[]{:S(2)}) copy-start(bf16[256,40]{0,1:T(8,128)(2,1)} %param.29) | copy-start | bytes 61444
  108.7 20.8 %copy-start.24 = (f32[40]{0:T(128)S(1)}, f32[40]{0:T(128)}, u32[]{:S(2)}) copy-start(f32[40]{0:T(128)} %param.31) | copy-start | bytes 484
  120.3 35.9 %all-to-all-start.1 = ((bf16[128,64,128]{2,1,0:T(8,128)(2,1)}), bf16[128,64,128]{2,1,0:T(8,128)(2,1)S(1)}, u32[]{:S(2)}, u32[]{:S(2)}) async-start(bf16[128,64,128]{2,1,0:T(8,128)(2,1)} %send_2.1), calls=%async_computation.1 | async-start | bytes 4194304 | tf_op jit(solution)/shard_map/all_to_all | solution.py:293
  156.2 1.3 copy-start.5
  209.9 17.3 %copy-start.15 = (f32[12288]{0:T(1024)S(1)}, f32[12288]{0:T(1024)}, u32[]{:S(2)}) copy-start(f32[12288]{0:T(1024)} %param.18) | copy-start | bytes 147460
  210.0 17.3 %copy-start.19 = (s32[12288]{0:T(1024)S(1)}, s32[12288]{0:T(1024)}, u32[]{:S(2)}) copy-start(s32[12288]{0:T(1024)} %param.17) | copy-start | bytes 147460
  221.5 40.1 %all-to-all-start.2 = ((bf16[128,64,128]{2,1,0:T(8,128)(2,1)}), bf16[128,64,128]{2,1,0:T(8,128)(2,1)S(1)}, u32[]{:S(2)}, u32[]{:S(2)}) async-start(bf16[128,64,128]{2,1,0:T(8,128)(2,1)} %send_3.1), calls=%async_computation.2 | async-start | bytes 4194304 | tf_op jit(solution)/shard_map/all_to_all | solution.py:293
  261.6 1.3 copy-start.6
  310.3 30.2 %copy-start.10 = (s32[8192]{0:T(1024)S(1)}, s32[8192]{0:T(1024)}, u32[]{:S(2)}) copy-start(s32[8192]{0:T(1024)} %reshape.190.idx_ref) | copy-start | bytes 98308
  310.3 36.8 %copy-start.11 = (bf16[256,256]{1,0:T(8,128)(2,1)S(1)}, bf16[256,256]{1,0:T(8,128)(2,1)}, u32[]{:S(2)}) copy-start(bf16[256,256]{1,0:T(8,128)(2,1)} %refs_6_.1) | copy-start | bytes 393220
  333.8 41.3 %all-to-all-start.3 = ((bf16[128,64,128]{2,1,0:T(8,128)(2,1)}), bf16[128,64,128]{2,1,0:T(8,128)(2,1)S(1)}, u32[]{:S(2)}, u32[]{:S(2)}) async-start(bf16[128,64,128]{2,1,0:T(8,128)(2,1)} %bitcast.60), calls=%async_computation.3 | async-start | bytes 4194304 | tf_op jit(solution)/shard_map/all_to_all | solution.py:293
  346.8 28.3 %copy-start.14 = (s32[8192]{0:T(1024)}, s32[8192]{0:T(1024)S(1)}, u32[]{:S(2)}) copy-start(s32[8192]{0:T(1024)S(1)} %get-tuple-element.109) | copy-start | bytes 98308
  375.1 1.3 copy-start.4
  429.6 13.3 %copy-start.12 = (bf16[256,256]{1,0:T(8,128)(2,1)S(1)}, bf16[256,256]{1,0:T(8,128)(2,1)}, u32[]{:S(2)}) copy-start(bf16[256,256]{1,0:T(8,128)(2,1)} %refs_5_.3) | copy-start | bytes 393220
  429.6 14.1 %copy-start.7 = (bf16[12288,128]{1,0:T(8,128)(2,1)S(1)}, bf16[12288,128]{1,0:T(8,128)(2,1)}, u32[]{:S(2)}) copy-start(bf16[12288,128]{1,0:T(8,128)(2,1)} %get-tuple-element.31.refs_2_) | copy-start | bytes 9437188
  429.6 71.8 %all-to-all-start.4 = ((bf16[128,64,256]{2,1,0:T(8,128)(2,1)}), bf16[128,64,256]{2,1,0:T(8,128)(2,1)}, u32[]{:S(2)}, u32[]{:S(2)}) async-start(bf16[128,64,256]{2,1,0:T(8,128)(2,1)} %bitcast.58), calls=%async_computation.4 | async-start | bytes 8388608 | tf_op jit(solution)/shard_map/all_to_all | solution.py:293
  442.9 5.5 copy-start.23
  442.9 6.1 %copy-start.22 = (f32[8,128]{1,0:T(8,128)S(1)}, f32[8,128]{1,0:T(8,128)}, u32[]{:S(2)}) copy-start(f32[8,128]{1,0:T(8,128)} %get-tuple-element.40) | copy-start | bytes 12292
  449.1 12.6 %slice-start = ((s8[6291456]{0:T(1024)(128)(4,1)}), s8[2097152]{0:T(1024)(128)(4,1)S(1)}, s32[]{:S(2)}) async-start(s8[6291456]{0:T(1024)(128)(4,1)} %bitcast.55), calls=%async_computation.7 | async-start | bytes 4194304
  454.9 6.7 %slice-start.1 = ((s8[6291456]{0:T(1024)(128)(4,1)}), s8[4194304]{0:T(1024)(128)(4,1)S(1)}, s32[]{:S(2)}) async-start(s8[6291456]{0:T(1024)(128)(4,1)} %bitcast.55), calls=%async_computation.8 | async-start | bytes 8388608
  461.7 4.8 copy-start.20
  501.5 25.8 %copy-start.2 = (bf16[12288,128]{1,0:T(8,128)(2,1)S(1)}, bf16[12288,128]{1,0:T(8,128)(2,1)}, u32[]{:S(2)}) copy-start(bf16[12288,128]{1,0:T(8,128)(2,1)} %get-tuple-element.27.src_ref) | copy-start | bytes 9437188
  527.2 4.6 copy-start
  527.2 5.5 copy-start.1
  532.7 2.2 copy-start.21

commit v3 on v2

v3 whole, which is shorter than its diff:
```python
import math

import jax
import jax.numpy as jnp
from jax import lax
from jax.experimental import pallas as pl
from jax.experimental.pallas import tpu as pltpu
from jax.sharding import PartitionSpec as P

GROUP_AXIS = 'gp'
LANES = 128
SPREAD = 40
BLOCK = 128
GROUP = 8
TAIL = 8
F32 = jnp.float32
BF16 = jnp.bfloat16
VMEM_LIMIT = 60 * 2 ** 20

SMEM_SPEC = pl.BlockSpec(memory_space=pltpu.SMEM)
HBM_SPEC = pl.BlockSpec(memory_space=pltpu.HBM)


def whole_spec(shape):
    return pl.BlockSpec(shape, lambda i: (0,) * len(shape))


def row_spec(rows, width):
    return pl.BlockSpec((rows, width), lambda i: (i, 0))


def params(limit=VMEM_LIMIT):
    return pltpu.CompilerParams(vmem_limit_bytes=limit, dimension_semantics=('arbitrary',))


def cost(micros):
    return pl.CostEstimate(flops=int(micros * 4e6), bytes_accessed=int(micros * 1e6), transcendentals=0)


def mm(a, b):
    return jnp.dot(a, b, preferred_element_type=F32)


def tile_linear(row):
    return ((row >> 3) << 4) | (row & 7)


def put_rows(tab, row0, x, nc):
    rows = x.shape[0]
    if nc == 1:
        tab[pl.ds(pl.multiple_of(row0, 8), rows), :] = x
    else:
        for g in range(rows // 8):
            for c in range(nc):
                at = pl.multiple_of((row0 + g * 8) * nc + c * 8, 8)
                tab[pl.ds(at, 8), :] = x[g * 8:g * 8 + 8, c * LANES:(c + 1) * LANES]


def fetch(src, stage, sem, parts):
    rows = src.shape[0] // parts
    copies = [pltpu.make_async_copy(src.at[pl.ds(k * rows, rows)], stage.at[pl.ds(k * rows, rows)], sem.at[k])
              for k in range(parts)]
    for c in copies:
        c.start()
    return copies


def unpack(copies, stage, tab, row0, nc):
    rows = stage.shape[0] // len(copies)
    step = next(d for d in (128, 96, 64, 32, 16) if rows % d == 0)
    for p, c in enumerate(copies):
        c.wait()

        def body(k, carry):
            at = pl.multiple_of(p * rows + k * step, step)
            put_rows(tab, row0 + at, stage[pl.ds(at, step), :].astype(F32), nc)
            return carry
        lax.fori_loop(0, rows // step, body, 0)


def group_of(blocks):
    return next(u for u in (GROUP, 4, 2) if blocks % u == 0)


def zero_rows(acc):
    rows = acc.shape[0]
    step = next(s for s in (256, 128, 64, 32, 16, 8) if rows % s == 0)

    def body(k, carry):
        acc[pl.ds(pl.multiple_of(k * step, step), step), :] = jnp.zeros((step, acc.shape[1]), F32)
        return carry
    lax.fori_loop(0, rows // step, body, 0)


def gather_16(idx, first, tab, nc):
    sub = lax.broadcasted_iota(jnp.int32, (8, LANES), 0)
    halves = [[None, None] for _ in range(nc)]
    for h in range(2):
        for k in range(8):
            at = idx[first + h * 8 + k]
            for c in range(nc):
                row = jnp.broadcast_to(tab[pl.ds(at + 8 * c, 1), :], (8, LANES))
                halves[c][h] = row if k == 0 else jnp.where(sub == k, row, halves[c][h])
    return [jnp.concatenate(halves[c], axis=0).astype(BF16) for c in range(nc)]


def segment_sums(meta, meta_at, idx, seg, tab, acc, bufs, nc, window, blocks):
    unroll = group_of(blocks)
    first_trip, end_trip, most = [meta[meta_at + 2 * blocks + k] for k in range(3)]

    def fill(b, buf):
        for g in range(BLOCK // 16):
            parts = gather_16(idx, b * BLOCK + g * 16, tab, nc)
            for c in range(nc):
                buf[g * 16:g * 16 + 16, c * LANES:(c + 1) * LANES] = parts[c]

    def sums(b, at, buf):
        rows = lax.broadcasted_iota(jnp.int32, (window, BLOCK), 0) + at
        return mm(jnp.where(rows == seg[b], 1.0, 0.0).astype(BF16), buf[...])

    def add(at, x):
        acc[pl.ds(pl.multiple_of(at, 8), window), :] += x

    fill(jnp.minimum(first_trip * unroll, blocks - 1), bufs[0])

    def body(t, carry):
        before = None
        for u in range(unroll):
            b = t * unroll + u
            now = (meta[meta_at + b], sums(b, meta[meta_at + b], bufs[u % 2]))
            fill(jnp.minimum(b + 1, blocks - 1), bufs[(u + 1) % 2])
            if before is not None:
                add(*before)
            before = now
        add(*before)
        return carry
    lax.fori_loop(first_trip, end_trip, body, 0)

    @pl.when(most > 1)
    def _():
        def again(b, carry):
            count = meta[meta_at + blocks + b]

            @pl.when(count > 1)
            def _():
                fill(b, bufs[0])

                def more(w, c):
                    at = meta[meta_at + b] + w * window
                    add(at, sums(b, at, bufs[0]))
                    return c
                lax.fori_loop(1, count, more, 0)
            return carry
        lax.fori_loop(first_trip * unroll, end_trip * unroll, again, 0)


def spread_lanes():
    return lax.broadcasted_iota(jnp.int32, (1, LANES), 1)


def split3(x):
    hi = x.astype(BF16).astype(F32)
    rest = x - hi
    mid = rest.astype(BF16).astype(F32)
    low = rest - mid
    lane = spread_lanes()
    out = jnp.where(lane < SPREAD, hi, jnp.where(lane < 2 * SPREAD, mid, low))
    return jnp.where(lane < 3 * SPREAD, out, 0.0).astype(BF16)


def pieces3(a):
    hi = a.astype(BF16)
    rest = a - hi.astype(F32)
    mid = rest.astype(BF16)
    low = (rest - mid.astype(F32)).astype(BF16)
    return jnp.concatenate([hi, mid, low], axis=1)


def fold3(a, folder):
    return mm(pieces3(a), folder)


def add_rows(ref, x):
    ref[...] += jnp.sum(x.reshape(x.shape[0] // 8, 8, x.shape[1]), axis=0)


def pick_rows(name, src, idx, peers, slots, mask):
    n = src.shape[0]
    per = math.gcd(peers, 32)
    extra = 0 if mask is None else TAIL
    parts = math.gcd(n // 128, 4)

    def kern(idx_ref, src_ref, *refs):
        if extra:
            mask_ref, out, tab, stage, sem, tail = refs
        else:
            out, tab, stage, sem = refs

        @pl.when(pl.program_id(0) == 0)
        def _():
            copies = fetch(src_ref, stage, sem, parts)
            if extra:
                total = jnp.sum(mask_ref[...], axis=(0, 1), keepdims=True)
                high = jnp.floor(total * (1.0 / LANES))
                first = lax.broadcasted_iota(jnp.int32, (TAIL, LANES), 0) == 0
                lane = lax.broadcasted_iota(jnp.int32, (TAIL, LANES), 1)
                digits = jnp.where(lane == 0, high, jnp.where(lane == 1, total - high * LANES, 0.0))
                tail[...] = jnp.where(first, digits, 0.0).astype(BF16)
            unpack(copies, stage, tab, 0, 1)
        first = pl.program_id(0) * (per * slots)

        def body(p, carry):
            for g in range(slots // 16):
                out[p, g * 16:g * 16 + 16, :] = gather_16(idx_ref, first + p * slots + g * 16, tab, 1)[0]
            if extra:
                out[p, slots:slots + extra, :] = tail[...]
            return carry
        lax.fori_loop(0, per, body, 0)

    operands = [idx, src] + ([mask] if extra else [])
    specs = [SMEM_SPEC, HBM_SPEC] + ([whole_spec(mask.shape)] if extra else [])
    return pl.pallas_call(
        kern, name=name, grid=(peers // per,),
        out_shape=jax.ShapeDtypeStruct((peers, slots + extra, LANES), BF16),
        in_specs=specs,
        out_specs=pl.BlockSpec((per, slots + extra, LANES), lambda i: (i, 0, 0)),
        scratch_shapes=([pltpu.VMEM((n, LANES), F32), pltpu.VMEM((n, LANES), BF16), pltpu.SemaphoreType.DMA((parts,))]
                        + ([pltpu.VMEM((TAIL, LANES), BF16)] if extra else [])),
        compiler_params=params(), cost_estimate=cost(10))(*operands)


def edge_call(name, edges, nc, table_rows, acc_rows, window, sources, build, hbm_in, blocked, fixed, outs, rows_out,
              tile, epilogue, micros, init=None, sub=256, limit=VMEM_LIMIT):
    meta, meta_at, idx, seg = edges
    blocks = seg.shape[0]
    width = nc * LANES
    nh, nb, nf, no, ns = len(hbm_in), len(blocked), len(fixed), len(outs), len(sources)
    acc_total = -(-(acc_rows + window) // 256) * 256
    parts = 4
    sub = math.gcd(sub, tile)

    def kern(meta_ref, idx_ref, seg_ref, *refs):
        hb, refs = refs[:nh], refs[nh:]
        bl, refs = refs[:nb], refs[nb:]
        fx, refs = refs[:nf], refs[nf:]
        out, refs = refs[:no], refs[no:]
        tab, acc, buf_0, buf_1, isem = refs[:5]
        stages, sems = refs[5:5 + ns], refs[5 + ns:]
        i = pl.program_id(0)

        @pl.when(i == 0)
        def _():
            copies = [fetch(h, st, sm, parts) for h, st, sm in zip(hb, stages, sems)]
            if init is None:
                zero_rows(acc)
            else:
                start = pltpu.make_async_copy(hb[init], acc.at[pl.ds(0, acc_rows), :], isem)
                start.start()
            for o, (_, _, sums) in zip(out, outs):
                if sums:
                    o[...] = jnp.zeros_like(o)
            build(copies, stages, tab, fx)
            if init is not None:
                start.wait()
            segment_sums(meta_ref, meta_at, idx_ref, seg_ref, tab, acc, (buf_0, buf_1), nc, window, blocks)
        for j in range(tile // sub):
            at = j * sub
            epilogue(acc[pl.ds(pl.multiple_of(i * tile + at, sub), sub), :], [r.at[pl.ds(at, sub), :] for r in bl], fx,
                     [o if sums else o.at[pl.ds(at, sub), :] for o, (_, _, sums) in zip(out, outs)])

    out_shape, out_specs = [], []
    for shape, dtype, sums in outs:
        out_shape.append(jax.ShapeDtypeStruct(shape, dtype))
        out_specs.append(whole_spec(shape) if sums else row_spec(tile, shape[1]))
    return pl.pallas_call(
        kern, name=name, grid=(rows_out // tile,), out_shape=out_shape,
        in_specs=([SMEM_SPEC, SMEM_SPEC, whole_spec(seg.shape)] + [HBM_SPEC] * nh
                  + [row_spec(tile, x.shape[1]) for x in blocked] + [whole_spec(x.shape) for x in fixed]),
        out_specs=out_specs,
        scratch_shapes=([pltpu.VMEM((table_rows * nc, LANES), F32), pltpu.VMEM((acc_total, width), F32),
                         pltpu.VMEM((BLOCK, width), BF16), pltpu.VMEM((BLOCK, width), BF16),
                         pltpu.SemaphoreType.DMA(())]
                        + [pltpu.VMEM(shape, BF16) for shape in sources]
                        + [pltpu.SemaphoreType.DMA((parts,)) for _ in sources]),
        compiler_params=params(limit), cost_estimate=cost(micros))(meta, idx, seg, *hbm_in, *blocked, *fixed)


def edge_meta(seg_first, seg_last, window, first_block, end_block):
    blocks = seg_first.shape[0]
    unroll = group_of(blocks)
    at = jnp.arange(blocks, dtype=jnp.int32)
    base = seg_first & ~7
    count = jnp.where((at >= first_block) & (at < end_block), (seg_last - base) // window + 1, 1)
    tail = jnp.stack([first_block // unroll, (end_block + unroll - 1) // unroll, jnp.max(count)])
    return [base, count, tail]


def join_meta(*metas):
    offsets, at = [], 0
    for m in metas:
        offsets.append(at)
        at += sum(x.shape[0] for x in m)
    return jnp.concatenate([x for m in metas for x in m]).astype(jnp.int32), offsets


def bits_for(n):
    return max(1, (n - 1).bit_length())


def spread3(w):
    w = jnp.pad(w, ((0, 0), (0, SPREAD - w.shape[1])))
    return jnp.pad(jnp.concatenate([w, w, w], axis=1), ((0, 0), (0, LANES - 3 * SPREAD)))


def lanes_pad(w):
    return jnp.pad(w, ((0, 0), (0, LANES - w.shape[1])))


def solution(mesh):
    peers = mesh.shape[GROUP_AXIS]

    def exchange(x):
        return lax.all_to_all(x, GROUP_AXIS, 0, 0, tiled=True)

    def device_step(features, labels, train_mask, send_idx, src_idx, dst_idx, inv_deg,
                    w_self_1, w_neigh_1, bias_1, w_self_2, w_neigh_2, bias_2,
                    w_self_3, w_neigh_3, bias_3):
        n = features.shape[0]
        slots = send_idx.shape[1]
        halo = peers * slots
        edges = src_idx.shape[0]
        hidden = w_self_1.shape[1]
        classes = w_self_3.shape[1]
        send_flat = send_idx.reshape(-1)
        tile = min(1024, n)
        slot_bits = bits_for(halo)
        dst_bits = bits_for(n)
        table = n + halo

        blocks = edges // BLOCK
        halo_blocks = halo // BLOCK
        zero = jnp.int32(0)
        win_e, win_h, win_r = 176, 144, 240
        owned = jnp.sum((src_idx < n).astype(jnp.int32))
        near_end = (owned + BLOCK - 1) // BLOCK
        far_start = owned // BLOCK

        src_bits = bits_for(table)
        far_bit = dst_bits + src_bits
        by_dst = lax.sort(((src_idx >= n).astype(jnp.int32) << far_bit) | (dst_idx << src_bits) | src_idx, is_stable=False)
        src_f = by_dst & ((1 << src_bits) - 1)
        dst_f = (by_dst >> src_bits) & ((1 << dst_bits) - 1)
        is_far = src_f >= n
        src_near = jnp.minimum(src_f, n - 1)
        src_far = jnp.maximum(src_f - n, 0)
        seg_near = jnp.where(is_far, -1, dst_f).reshape(blocks, 1, BLOCK)
        seg_far = jnp.where(is_far, dst_f, -1).reshape(blocks, 1, BLOCK)
        first, last = dst_f[::BLOCK], dst_f[BLOCK - 1::BLOCK]
        meta_f, (near_at, far_at) = join_meta(
            edge_meta(first, jnp.where(is_far[BLOCK - 1::BLOCK], n - 1, last), win_e, zero, near_end),
            edge_meta(jnp.where(is_far[::BLOCK], first, 0), last, win_e, far_start, jnp.int32(blocks)))

        keys = jnp.concatenate([(src_idx << dst_bits) | dst_idx,
                                (1 << 30) | (send_flat << slot_bits) | jnp.arange(halo, dtype=jnp.int32)])
        ordered = lax.sort(keys, is_stable=False)
        by_src, by_row = ordered[:edges], ordered[edges:] & ((1 << 30) - 1)
        src_s = by_src >> dst_bits
        dst_s = by_src & ((1 << dst_bits) - 1)
        row_s = by_row >> slot_bits
        slot_s = by_row & ((1 << slot_bits) - 1)
        first, last = src_s[::BLOCK], src_s[BLOCK - 1::BLOCK]
        meta_b, (own_at, halo_at, owner_at) = join_meta(
            edge_meta(jnp.minimum(first, n - 1), jnp.minimum(last, n - 1), win_e, zero, near_end),
            edge_meta(jnp.maximum(first - n, 0), jnp.maximum(last - n, 0), win_h, far_start, jnp.int32(blocks)),
            edge_meta(row_s[::BLOCK], row_s[BLOCK - 1::BLOCK], win_r, zero, jnp.int32(halo_blocks)))
        seg_o = src_s.reshape(blocks, 1, BLOCK)
        seg_h = seg_o - n
        seg_r = row_s.reshape(halo_blocks, 1, BLOCK)
        dst_wide = tile_linear(dst_s)

        inv = jnp.broadcast_to(inv_deg[:, None], (n, LANES))
        b1 = bias_1.reshape(1, -1)
        b2 = bias_2.reshape(1, -1)
        lane = jnp.arange(LANES, dtype=jnp.int32)
        used = lane < 3 * SPREAD
        folder = jnp.tile(((lane[:, None] % SPREAD == lane[None, :] % SPREAD) & used[:, None] & used[None, :]).astype(BF16),
                          (3, 1))
        b3 = jnp.where(lane < 3 * SPREAD, spread3(bias_3.reshape(1, -1)), -1e30)
        if classes < SPREAD:
            b3 = jnp.where(lane % SPREAD < classes, b3, -1e30)
        target = jnp.where(lane[None, :] < 3 * SPREAD,
                           train_mask[:, None] * (1.0 + (labels[:, None] == lane[None, :] % SPREAD)), 0.0).astype(BF16)
        ws3, wn3 = spread3(w_self_3), spread3(w_neigh_3)
        ws3_t, wn3_t = lanes_pad(w_self_3).T, lanes_pad(w_neigh_3).T

        def rows_of(nc):
            def build(copies, stages, tab, fx):
                unpack(copies[0], stages[0], tab, 0, nc)
            return build

        def epi_plain(a, bl, fx, out):
            out[0][...] = a

        def near_sums(name, nc, idx, rows, also):
            return edge_call(name, (meta_f, near_at, idx, seg_near), nc, n, n, win_e, [rows.shape], rows_of(nc),
                             [rows] + also, [], [], [((n, nc * LANES), F32, False)], n, tile, epi_plain, 20, sub=tile)[0]

        out_1 = pick_rows('send_1', features, send_flat, peers, slots, train_mask.reshape(-1, LANES))
        got_1 = exchange(out_1)
        near_1 = near_sums('near_1', 1, src_near, features, [inv])
        counts = got_1[:, slots, :2].astype(F32)
        total = jnp.sum(counts[:, 0]) * LANES + jnp.sum(counts[:, 1])

        def build_1(copies, stages, tab, fx):
            per = peers // len(copies[0])
            some = math.gcd(per, 8)
            for p in range(len(copies[0])):
                copies[0][p].wait()

                def body(k, carry):
                    q = p * per + k * some
                    rows = stages[0][pl.ds(q, some), :slots, :].reshape(some * slots, LANES)
                    put_rows(tab, q * slots, rows.astype(F32), 1)
                    return carry
                lax.fori_loop(0, per // some, body, 0)

        def epi_1(a, bl, fx, out):
            mean = (a * bl[1][...]).astype(BF16)
            z = mm(bl[0][...], fx[0][...]) + mm(mean, fx[1][...]) + fx[2][...]
            out[0][...] = mean
            out[1][...] = jnp.maximum(z, 0.0).astype(BF16)

        mean_1, hidden_1 = edge_call(
            'layer_1', (meta_f, far_at, src_far, seg_far), 1, halo, n, win_e, [(peers, slots + TAIL, LANES)], build_1,
            [got_1, near_1], [features, inv], [w_self_1, w_neigh_1, b1],
            [((n, LANES), BF16, False), ((n, hidden), BF16, False)], n, tile, epi_1, 25, init=1)

        out_2 = pick_rows('send_2', mean_1, send_flat, peers, slots, None)
        got_2 = exchange(out_2)
        near_2 = near_sums('near_2', 2, tile_linear(src_near), hidden_1, [])

        def build_2(copies, stages, tab, fx):
            per = peers // len(copies[0])
            some = math.gcd(per, 8)
            for p in range(len(copies[0])):
                copies[0][p].wait()
                copies[1][p].wait()

                def body(k, carry):
                    q = p * per + k * some
                    f = stages[0][pl.ds(q, some), :slots, :].reshape(some * slots, LANES)
                    m = stages[1][pl.ds(q, some)].reshape(some * slots, LANES)
                    z = mm(f, fx[3][...]) + mm(m, fx[4][...]) + fx[5][...]
                    put_rows(tab, q * slots, jnp.maximum(z, 0.0).astype(BF16).astype(F32), 2)
                    return carry
                lax.fori_loop(0, per // some, body, 0)

        def epi_2(a, bl, fx, out):
            scale = bl[1][...]
            mean = (a * jnp.concatenate([scale, scale], axis=1)).astype(BF16)
            z = mm(bl[0][...], fx[0][...]) + mm(mean, fx[1][...]) + fx[2][...]
            h = jnp.maximum(z, 0.0).astype(BF16)
            out[0][...] = mean
            out[1][...] = h
            both = mm(h, fx[6][...])
            out[2][...] = split3(both[:, :LANES])
            out[3][...] = both[:, LANES:]

        mean_2, hidden_2, proj, logits_self = edge_call(
            'layer_2', (meta_f, far_at, tile_linear(src_far), seg_far), 2, halo, n, win_e,
            [(peers, slots + TAIL, LANES), (peers, slots, LANES)], build_2, [got_1, got_2, near_2],
            [hidden_1, inv], [w_self_2, w_neigh_2, b2, w_self_1, w_neigh_1, b1, jnp.concatenate([wn3, ws3], axis=1)],
            [((n, hidden), BF16, False), ((n, hidden), BF16, False), ((n, LANES), BF16, False),
             ((n, LANES), F32, False)], n, tile, epi_2, 40, init=2, sub=1024)

        out_3 = pick_rows('send_3', proj, send_flat, peers, slots, None)
        got_3 = exchange(out_3).reshape(halo, LANES)
        near_3 = near_sums('near_3', 1, src_near, proj, [target])
        inv_total = (1.0 / total).reshape(1, 1)

        def epi_3(a, bl, fx, out):
            scale = bl[1][...]
            z = bl[0][...] + fold3(a * scale, fx[2][...]) + fx[0][...]
            lane = spread_lanes()
            z = jnp.where(lane < 3 * SPREAD, z, -1e30)
            top = jnp.max(z, axis=1, keepdims=True)
            e = jnp.where(lane < SPREAD, jnp.exp(z - top), 0.0)
            lse = top + jnp.log(jnp.sum(e, axis=1, keepdims=True))
            t = bl[2][...].astype(F32)
            hit = t > 1.5
            d = jnp.where(t > 0.5, jnp.exp(z - lse) - jnp.where(hit, 1.0, 0.0), 0.0) * fx[1][...]
            db = d.astype(BF16)
            out[0][...] = db
            out[1][...] = split3(db.astype(F32) * scale)
            add_rows(out[2], d)
            add_rows(out[3], jnp.where(hit & (lane < SPREAD), lse - z, 0.0))

        d_bf_3, scaled_3, g_b3, loss_parts = edge_call(
            'layer_3', (meta_f, far_at, src_far, seg_far), 1, halo, n, win_e, [(halo, LANES)], rows_of(1), [got_3, near_3],
            [logits_self, inv, target], [b3, jnp.broadcast_to(inv_total, (1, LANES)), folder],
            [((n, LANES), BF16, False), ((n, LANES), BF16, False), ((8, LANES), F32, True), ((8, LANES), F32, True)],
            n, tile, epi_3, 30, init=1, sub=1024)

        def epi_b3h(a, bl, fx, out):
            out[0][...] = split3(fold3(a, fx[0][...]))

        tile_h = min(1024, halo)
        back_3 = edge_call('back_3_halo', (meta_b, halo_at, dst_s, seg_h), 1, n, halo, win_h, [(n, LANES)], rows_of(1),
                           [scaled_3], [], [folder], [((halo, LANES), BF16, False)], halo, tile_h, epi_b3h, 15, sub=1024)[0]
        ret_3 = exchange(back_3.reshape(peers, slots, LANES)).reshape(halo, LANES)
        own_3 = edge_call('back_3_own', (meta_b, own_at, dst_s, seg_o), 1, n, n, win_e, [(n, LANES)], rows_of(1),
                          [scaled_3], [], [], [((n, LANES), F32, False)], n, tile, epi_plain, 20, sub=tile)[0]

        def epi_o3(a, bl, fx, out):
            tb = fold3(a, fx[2][...]).astype(BF16)
            d_h = mm(jnp.concatenate([bl[0][...], tb], axis=1), fx[0][...])
            d_pre = jnp.where(bl[1][...].astype(F32) > 0, d_h, 0.0)
            db = d_pre.astype(BF16)
            scale = bl[2][...]
            out[0][...] = tb
            out[1][...] = db
            out[2][...] = (mm(db, fx[1][...]) * jnp.concatenate([scale, scale], axis=1)).astype(BF16)
            add_rows(out[3], d_pre)

        tb_3, d_bf_2, scaled_2, g_b2 = edge_call(
            'owner_3', (meta_b, owner_at, slot_s, seg_r), 1, halo, n, win_r, [(halo, LANES)], rows_of(1), [ret_3, own_3],
            [d_bf_3, hidden_2, inv], [jnp.concatenate([ws3_t, wn3_t], axis=0), w_neigh_2.T, folder],
            [((n, LANES), BF16, False), ((n, hidden), BF16, False), ((n, hidden), BF16, False), ((8, hidden), F32, True)],
            n, tile, epi_o3, 30, init=1, sub=512)

        def epi_b2h(a, bl, fx, out):
            out[0][...] = a.astype(BF16)

        def epi_b2o(a, bl, fx, out):
            out[0][...] = a + mm(bl[0][...], fx[0][...])

        back_2 = edge_call('back_2_halo', (meta_b, halo_at, dst_wide, seg_h), 2, n, halo, win_h, [(n, hidden)], rows_of(2),
                           [scaled_2], [], [], [((halo, hidden), BF16, False)], halo, tile_h, epi_b2h, 20)[0]
        ret_2 = exchange(back_2.reshape(peers, slots, hidden)).reshape(halo, hidden)
        own_2 = edge_call('back_2_own', (meta_b, own_at, dst_wide, seg_o), 2, n, n, win_e, [(n, hidden)], rows_of(2),
                          [scaled_2], [d_bf_2], [w_self_2.T], [((n, hidden), F32, False)], n, tile, epi_b2o, 30)[0]

        def epi_o2(a, bl, fx, out):
            d_pre = jnp.where(bl[0][...].astype(F32) > 0, a, 0.0)
            out[0][...] = d_pre.astype(BF16)
            add_rows(out[1], d_pre)

        d_bf_1, g_b1 = edge_call(
            'owner_2', (meta_b, owner_at, tile_linear(slot_s), seg_r), 2, halo, n, win_r, [(halo, hidden)], rows_of(2),
            [ret_2, own_2], [hidden_1], [], [((n, hidden), BF16, False), ((8, hidden), F32, True)], n, tile, epi_o2, 25,
            init=1)

        def contract(a, b):
            return jnp.einsum('nd,ne->de', a, b, preferred_element_type=F32)

        parts = [contract(features, d_bf_1), contract(mean_1, d_bf_1), jnp.sum(g_b1, axis=0),
                 contract(hidden_1, d_bf_2), contract(mean_2, d_bf_2), jnp.sum(g_b2, axis=0),
                 contract(hidden_2, d_bf_3)[:, :classes], contract(hidden_2, tb_3)[:, :classes],
                 jnp.sum(g_b3, axis=0)[:classes], jnp.sum(loss_parts).reshape(1)]
        sizes = [p.size for p in parts]
        whole = sum(sizes)
        share = -(-whole // (peers * LANES)) * LANES
        flat = jnp.concatenate([p.reshape(-1) for p in parts] + [jnp.zeros((share * peers - whole,), F32)])
        mine = jnp.sum(exchange(flat.reshape(peers, share)), axis=0)
        full = exchange(jnp.broadcast_to(mine, (peers, share))).reshape(-1)
        outs, at = [], 0
        for p, size in zip(parts, sizes):
            outs.append(full[at:at + size].reshape(p.shape))
            at += size
        return (outs[-1][0] / total,) + tuple(outs[:-1])

    sharded = P(GROUP_AXIS)
    whole = P()
    return jax.shard_map(device_step, mesh=mesh,
                         in_specs=(sharded,) * 7 + (whole,) * 9,
                         out_specs=(whole,) * 10, check_vma=False)
```

time: 607 us -> 589 us (0.970)
  waiting for transfers between devices: 76 us -> 16.2 us
  Pallas kernels: 331 us -> 365 us
  starting transfers between devices: 41.6 us -> 51.1 us
    all_to_all x5, waiting for transfers between devices: 76 us -> 16.2 us  [exchange(): return lax.all_to_all(x, GROUP_AXIS, 0, 0, tiled=True)]
    pallas_call x9 -> x12, Pallas kernels: 297 us -> 330 us  [edge_call(): pl.pallas_call(kern, name=name, grid=(rows_out // tile,), out_shape=out_s...]
    all_to_all x5, starting transfers between devices: 41.6 us -> 51.1 us  [exchange(): return lax.all_to_all(x, GROUP_AXIS, 0, 0, tiled=True)]
  transfers between devices with their start and end apart: 5 -> 5, of which waited for: 4 -> 3; matrix products, arithmetic and copies ran while one was open for 10% -> 11% of each run, Pallas kernels for 9% -> 22%
where the time goes in v3:
time: 589 us; the launch traced here: 579 us
  Pallas kernels  365 us (62%)
  starting transfers between devices  51.1 us (9%)
  blocking collectives  45.8 us (8%)
  other arithmetic  34.7 us (6%)
  local copies, waits for them, and re-layouts  30.1 us (5%)
  matrix products  27.5 us (5%)
  waiting for transfers between devices  16.2 us (3%)
  between operations  8.2 us (1%)
    pallas_call x12, Pallas kernels, edge_call(): pl.pallas_call(kern, name=name, grid=(rows_out // tile,), out_shape=out_s...  330 us
    all_to_all x5, starting transfers between devices, exchange(): return lax.all_to_all(x, GROUP_AXIS, 0, 0, tiled=True)  51.1 us
    all_to_all x2, blocking collectives, exchange(): return lax.all_to_all(x, GROUP_AXIS, 0, 0, tiled=True)  45.8 us
    pallas_call x3, Pallas kernels, pick_rows(): pl.pallas_call(kern, name=name, grid=(peers // per,), out_shape=jax.Shape...  34.9 us
    dot_general x4, matrix products, contract(): return jnp.einsum('nd,ne->de', a, b, preferred_element_type=F32)  17.2 us
    all_to_all x5, waiting for transfers between devices, exchange(): return lax.all_to_all(x, GROUP_AXIS, 0, 0, tiled=True)  16.2 us
  transfers between devices with their start and end apart: 5, of which 3 were waited for; matrix products, arithmetic and copies ran while one was open for 11% of the time, Pallas kernels for 22%

profile of v3, /device:TPU:1, one launch (start us, length us, event | category | flops | bytes accessed | tf_op | source)
XLA Modules:
  0.0 578.8 jit_solution(5553466445172937536)
XLA Ops:
  0.7 0.9 copy.76
  2.3 11.7 %send_1.1 = bf16[128,72,128]{2,1,0:T(8,128)(2,1)} custom-call(s32[8192]{0:T(1024)} %reshape.257.idx_ref, bf16[12288,128]{1,0:T(8,128)(2,1)} %refs_2_.1, f32[96,128]{1,0:T(8,128)} %bitcast.91), custom_call_target="tpu_custom_call" | custom-call | flops 40000000 | bytes 10000000 | tf_op jit(solution)/shard_map/send_1/pallas_call | solution.py:222
  14.0 11.5 %all-to-all-start = ((bf16[128,72,128]{2,1,0:T(8,128)(2,1)}), bf16[128,72,128]{2,1,0:T(8,128)(2,1)S(1)}, u32[]{:S(2)}, u32[]{:S(2)}) async-start(bf16[128,72,128]{2,1,0:T(8,128)(2,1)} %send_1.1), calls=%async_computation | async-start | bytes 4718592 | tf_op jit(solution)/shard_map/all_to_all | solution.py:323
  26.2 8.6 %sort.15 = s32[24576]{0:T(1024)S(1)} sort(s32[24576]{0:T(1024)S(1)} %get-tuple-element.105), dimensions={0}, to_apply=%region_5.6 | sort | flops 368640 | bytes 196608 | tf_op jit(solution)/shard_map/sort | solution.py:350
  34.8 0.8 broadcast_select_fusion
  40.0 7.3 %sort.14 = s32[32768]{0:T(1024)S(1)} sort(s32[32768]{0:T(1024)S(1)} %pad_add_fusion), dimensions={0}, to_apply=%region_0.0 | sort | flops 491520 | bytes 262144 | tf_op jit(solution)/shard_map/sort | solution.py:365
  49.7 2.0 concatenate.29.meta_ref
  51.7 3.8 broadcast_in_dim.60.refs_1_.refs_3_.refs_4_
  55.5 23.8 %near_1.1.refs_1_ = f32[12288,128]{1,0:T(8,128)} custom-call(s32[774]{0:T(1024)} %concatenate.29.meta_ref, s32[24576]{0:T(1024)} %get-tuple-element.115.idx_ref, s32[192,1,128]{2,1,0:T(1,128)} %bitcast.68, bf16[12288,128]{1,0:T(8,128)(2,1)} %refs_2_.1, f32[12288,128]{1,0:T(8,128)} %broadcast_in_dim.60.refs_1_.refs_3_.refs_4_), custom_call_target="tpu_custom_call" | custom-call | flops 80000000 | bytes 20000000 | tf_op jit(solution)/shard_map/near_1/pallas_call | solution.py:275
  79.3 1.4 copy-done.3
  80.6 30.1 %layer_1.1 = (bf16[12288,128]{1,0:T(8,128)(2,1)}, bf16[12288,256]{1,0:T(8,128)(2,1)}) custom-call(s32[774]{0:T(1024)} %concatenate.29.meta_ref, s32[24576]{0:T(1024)} %get-tuple-element.118.idx_ref, s32[192,1,128]{2,1,0:T(1,128)} %bitcast.74, bf16[128,72,128]{2,1,0:T(8,128)(2,1)} %copy-done.3, f32[12288,128]{1,0:T(8,128)} %near_1.1.refs_1_, ...), custom_call_target="tpu_custom_call" | custom-call | flops 100000000 | bytes 25000000 | tf_op jit(solution)/shard_map/layer_1/pallas_call | solution.py:275
  110.8 11.5 %send_2.1 = bf16[128,64,128]{2,1,0:T(8,128)(2,1)} custom-call(s32[8192]{0:T(1024)} %reshape.257.idx_ref, bf16[12288,128]{1,0:T(8,128)(2,1)} %get-tuple-element.26.src_ref), custom_call_target="tpu_custom_call" | custom-call | flops 40000000 | bytes 10000000 | tf_op jit(solution)/shard_map/send_2/pallas_call | solution.py:222
  122.4 11.2 %all-to-all-start.1 = ((bf16[128,64,128]{2,1,0:T(8,128)(2,1)}), bf16[128,64,128]{2,1,0:T(8,128)(2,1)S(1)}, u32[]{:S(2)}, u32[]{:S(2)}) async-start(bf16[128,64,128]{2,1,0:T(8,128)(2,1)} %send_2.1), calls=%async_computation.1 | async-start | bytes 4194304 | tf_op jit(solution)/shard_map/all_to_all | solution.py:323
  135.4 2.6 concatenate.28.meta_ref
  139.6 26.2 %near_2.1.refs_2_ = f32[12288,256]{1,0:T(8,128)} custom-call(s32[774]{0:T(1024)} %concatenate.29.meta_ref, s32[24576]{0:T(1024)} %get-tuple-element.114.idx_ref, s32[192,1,128]{2,1,0:T(1,128)} %bitcast.69, bf16[12288,256]{1,0:T(8,128)(2,1)} %get-tuple-element.27.refs_0_.refs_3_.refs_2_), custom_call_target="tpu_custom_call" | custom-call | flops 80000000 | bytes 20000000 | tf_op jit(solution)/shard_map/near_2/pallas_call | solution.py:275
  165.8 2.1 all-to-all-done.1.refs_1_
  167.8 1.3 copy-done.4
  169.1 37.4 %layer_2.1 = (bf16[12288,256]{1,0:T(8,128)(2,1)}, bf16[12288,256]{1,0:T(8,128)(2,1)}, bf16[12288,128]{1,0:T(8,128)(2,1)}, f32[12288,128]{1,0:T(8,128)}) custom-call(s32[774]{0:T(1024)} %concatenate.29.meta_ref, s32[24576]{0:T(1024)} %get-tuple-element.116.idx_ref, s32[192,1,128]{2,1,0:T(1,128)} %bitcast.75, bf16[128,72,128]{2,1,0:T(8,128)(2,1)} %copy-done.3, ...), custom_call_target="tpu_custom_call" | custom-call | flops 160000000 | bytes 40000000 | tf_op jit(solution)/shard_map/layer_2/pallas_call | solution.py:275
  206.6 11.6 %send_3.1 = bf16[128,64,128]{2,1,0:T(8,128)(2,1)} custom-call(s32[8192]{0:T(1024)} %reshape.257.idx_ref, bf16[12288,128]{1,0:T(8,128)(2,1)} %get-tuple-element.28.src_ref.refs_0_), custom_call_target="tpu_custom_call" | custom-call | flops 40000000 | bytes 10000000 | tf_op jit(solution)/shard_map/send_3/pallas_call | solution.py:222
  218.2 9.5 %all-to-all-start.2 = ((bf16[128,64,128]{2,1,0:T(8,128)(2,1)}), bf16[128,64,128]{2,1,0:T(8,128)(2,1)S(1)}, u32[]{:S(2)}, u32[]{:S(2)}) async-start(bf16[128,64,128]{2,1,0:T(8,128)(2,1)} %send_3.1), calls=%async_computation.2 | async-start | bytes 4194304 | tf_op jit(solution)/shard_map/all_to_all | solution.py:323
  227.7 6.7 %select_convert_fusion.refs_1_.refs_4_ = bf16[12288,128]{1,0:T(8,128)(2,1)} fusion(s32[128]{0:T(128)S(1)} %and_select_fusion, f32[12288]{0:T(1024)S(1)} %copy-done.13, s32[12288]{0:T(1024)S(1)} %copy-done.19, pred[128]{0:T(512)(128)(4,1)S(1)} %iota_compare_fusion.2), kind=kLoop, calls=%fused_computation | loop fusion | flops 9437184 | bytes 3244672 | tf_op jit(solution)/shard_map/convert_element_type | solution.py:392
  234.3 1.0 slice_convert_fusion
  237.4 23.3 %near_3.1.refs_1_ = f32[12288,128]{1,0:T(8,128)} custom-call(s32[774]{0:T(1024)} %concatenate.29.meta_ref, s32[24576]{0:T(1024)} %get-tuple-element.115.idx_ref, s32[192,1,128]{2,1,0:T(1,128)} %bitcast.70, bf16[12288,128]{1,0:T(8,128)(2,1)} %get-tuple-element.28.src_ref.refs_0_, bf16[12288,128]{1,0:T(8,128)(2,1)} %select_convert_fusion.refs_1_.refs_4_), custom_call_target="tpu_custom_call" | custom-call | flops 80000000 | bytes 20000000 | tf_op jit(solution)/shard_map/near_3/pallas_call | solution.py:275
  261.3 0.8 tile.17
  262.0 33.9 %layer_3.1 = (bf16[12288,128]{1,0:T(8,128)(2,1)}, bf16[12288,128]{1,0:T(8,128)(2,1)}, f32[8,128]{1,0:T(8,128)}, f32[8,128]{1,0:T(8,128)}) custom-call(s32[774]{0:T(1024)} %concatenate.29.meta_ref, s32[24576]{0:T(1024)} %get-tuple-element.118.idx_ref, s32[192,1,128]{2,1,0:T(1,128)} %bitcast.76, bf16[8192,128]{1,0:T(8,128)(2,1)} %bitcast.62, ...), custom_call_target="tpu_custom_call" | custom-call | flops 120000000 | bytes 30000000 | tf_op jit(solution)/shard_map/layer_3/pallas_call | solution.py:275
  296.0 22.0 %back_3_halo.1 = bf16[8192,128]{1,0:T(8,128)(2,1)} custom-call(s32[905]{0:T(1024)} %concatenate.28.meta_ref, s32[24576]{0:T(1024)} %get-tuple-element.107.idx_ref, s32[192,1,128]{2,1,0:T(1,128)} %bitcast.81, bf16[12288,128]{1,0:T(8,128)(2,1)} %get-tuple-element.30.refs_0_, bf16[384,128]{1,0:T(8,128)(2,1)} %bitcast.72), custom_call_target="tpu_custom_call" | custom-call | flops 60000000 | bytes 15000000 | tf_op jit(solution)/shard_map/back_3_halo/pallas_call | solution.py:275
  317.9 12.0 %all-to-all-start.3 = ((bf16[128,64,128]{2,1,0:T(8,128)(2,1)}), bf16[128,64,128]{2,1,0:T(8,128)(2,1)S(1)}, u32[]{:S(2)}, u32[]{:S(2)}) async-start(bf16[128,64,128]{2,1,0:T(8,128)(2,1)} %bitcast.61), calls=%async_computation.3 | async-start | bytes 4194304 | tf_op jit(solution)/shard_map/all_to_all | solution.py:323
  331.4 23.3 %back_3_own.1.refs_1_ = f32[12288,128]{1,0:T(8,128)} custom-call(s32[905]{0:T(1024)} %concatenate.28.meta_ref, s32[24576]{0:T(1024)} %get-tuple-element.107.idx_ref, s32[192,1,128]{2,1,0:T(1,128)} %bitcast.79, bf16[12288,128]{1,0:T(8,128)(2,1)} %get-tuple-element.30.refs_0_), custom_call_target="tpu_custom_call" | custom-call | flops 80000000 | bytes 20000000 | tf_op jit(solution)/shard_map/back_3_own/pallas_call | solution.py:275
  354.7 9.5 %all-to-all-done.3 = bf16[128,64,128]{2,1,0:T(8,128)(2,1)S(1)} async-done(((bf16[128,64,128]{2,1,0:T(8,128)(2,1)}), bf16[128,64,128]{2,1,0:T(8,128)(2,1)S(1)}, u32[]{:S(2)}, u32[]{:S(2)}) %all-to-all-start.3) | async-done | bytes 2097184 | tf_op jit(solution)/shard_map/all_to_all | solution.py:323
  364.2 1.3 copy-done.5
  365.6 30.6 %owner_3.1 = (bf16[12288,128]{1,0:T(8,128)(2,1)}, bf16[12288,256]{1,0:T(8,128)(2,1)}, bf16[12288,256]{1,0:T(8,128)(2,1)}, f32[8,256]{1,0:T(8,128)}) custom-call(s32[905]{0:T(1024)} %concatenate.28.meta_ref, s32[8192]{0:T(1024)} %get-tuple-element.111.idx_ref, s32[64,1,128]{2,1,0:T(1,128)} %bitcast.89, bf16[8192,128]{1,0:T(8,128)(2,1)} %bitcast.60, ...), custom_call_target="tpu_custom_call" | custom-call | flops 120000000 | bytes 30000000 | tf_op jit(solution)/shard_map/owner_3/pallas_call | solution.py:275
  396.2 21.7 %back_2_halo.1 = bf16[8192,256]{1,0:T(8,128)(2,1)} custom-call(s32[905]{0:T(1024)} %concatenate.28.meta_ref, s32[24576]{0:T(1024)} %get-tuple-element.108.idx_ref, s32[192,1,128]{2,1,0:T(1,128)} %bitcast.82, bf16[12288,256]{1,0:T(8,128)(2,1)} %get-tuple-element.33.refs_0_), custom_call_target="tpu_custom_call" | custom-call | flops 80000000 | bytes 20000000 | tf_op jit(solution)/shard_map/back_2_halo/pallas_call | solution.py:275
  418.0 6.9 %all-to-all-start.4 = ((bf16[128,64,256]{2,1,0:T(8,128)(2,1)}), bf16[128,64,256]{2,1,0:T(8,128)(2,1)}, u32[]{:S(2)}, u32[]{:S(2)}) async-start(bf16[128,64,256]{2,1,0:T(8,128)(2,1)} %bitcast.59), calls=%async_computation.4 | async-start | bytes 8388608 | tf_op jit(solution)/shard_map/all_to_all | solution.py:323
  425.7 4.6 fusion.2
  431.1 5.7 fusion
  436.9 6.6 %convolution_bitcast_fusion = f32[32,2,8,128]{3,2,1,0:T(8,128)S(1)} fusion(bf16[12288,256]{1,0:T(8,128)(2,1)} %get-tuple-element.37, bf16[12288,256]{1,0:T(8,128)(2,1)} %get-tuple-element.34.refs_1_), kind=kOutput, calls=%fused_computation.5 | convolution fusion | flops 1610612736 | bytes 12845056 | tf_op jit(solution)/shard_map/nd,ne->de/dot_general | solution.py:554
  443.7 4.6 convolution_bitcast_fusion.1
  448.4 30.4 %back_2_own.1.refs_1_ = f32[12288,256]{1,0:T(8,128)} custom-call(s32[905]{0:T(1024)} %concatenate.28.meta_ref, s32[24576]{0:T(1024)} %get-tuple-element.108.idx_ref, s32[192,1,128]{2,1,0:T(1,128)} %bitcast.80, bf16[12288,256]{1,0:T(8,128)(2,1)} %get-tuple-element.33.refs_0_, bf16[12288,256]{1,0:T(8,128)(2,1)} %get-tuple-element.34.refs_1_, ...), custom_call_target="tpu_custom_call" | custom-call | flops 120000000 | bytes 30000000 | tf_op jit(solution)/shard_map/back_2_own/pallas_call | solution.py:275
  478.9 4.6 all-to-all-done.4
  483.5 27.6 %owner_2.1 = (bf16[12288,256]{1,0:T(8,128)(2,1)}, f32[8,256]{1,0:T(8,128)}) custom-call(s32[905]{0:T(1024)} %concatenate.28.meta_ref, s32[8192]{0:T(1024)} %get-tuple-element.112.idx_ref, s32[64,1,128]{2,1,0:T(1,128)} %bitcast.90, bf16[8192,256]{1,0:T(8,128)(2,1)} %bitcast.25.refs_0_, f32[12288,256]{1,0:T(8,128)} %back_2_own.1.refs_1_, ...), custom_call_target="tpu_custom_call" | custom-call | flops 100000000 | bytes 25000000 | tf_op jit(solution)/shard_map/owner_2/pallas_call | solution.py:275
  511.1 4.1 convolution_bitcast_fusion.2
  515.7 0.9 copy-done.1
  516.6 1.9 convolution_bitcast_fusion.3
  518.9 3.7 concatenate.35
  522.6 23.7 %all_to_all.40 = f32[128,1,1792]{2,1,0:T(1,128)S(1)} all-to-all(f32[128,1,1792]{2,1,0:T(1,128)S(1)} %bitcast.67), channel_id=1, replica_groups=mesh['gp'=128] {'gp'}, dimensions={0} | all-to-all | bytes 1835008 | tf_op jit(solution)/shard_map/all_to_all | solution.py:323
  547.3 22.1 %all_to_all.41 = f32[128,1,1792]{2,1,0:T(1,128)S(1)} all-to-all(f32[128,1,1792]{2,1,0:T(1,128)S(1)} %broadcast_in_dim.66), channel_id=1, replica_groups=mesh['gp'=128] {'gp'}, dimensions={0} | all-to-all | bytes 1835008 | tf_op jit(solution)/shard_map/all_to_all | solution.py:323
  569.4 2.2 reduce.3
  571.8 0.8 fusion.23
  (108 shorter events, 18.8 us)
Async XLA Ops:
  0.6 24.9 %copy-start.14 = (s32[24576]{0:T(1024)S(1)}, s32[24576]{0:T(1024)}, u32[]{:S(2)}) copy-start(s32[24576]{0:T(1024)} %param.20) | copy-start | bytes 294916
  0.7 24.9 %copy-start.15 = (s32[24576]{0:T(1024)S(1)}, s32[24576]{0:T(1024)}, u32[]{:S(2)}) copy-start(s32[24576]{0:T(1024)} %param.21) | copy-start | bytes 294916
  2.2 37.7 %copy-start.9 = (s32[8192]{0:T(1024)S(1)}, s32[8192]{0:T(1024)}, u32[]{:S(2)}) copy-start(s32[8192]{0:T(1024)} %reshape.257.idx_ref) | copy-start | bytes 98308
  2.3 49.4 %copy-start.18 = (f32[12288]{0:T(1024)S(1)}, f32[12288]{0:T(1024)}, u32[]{:S(2)}) copy-start(f32[12288]{0:T(1024)} %param.22) | copy-start | bytes 147460
  14.0 65.3 %all-to-all-start = ((bf16[128,72,128]{2,1,0:T(8,128)(2,1)}), bf16[128,72,128]{2,1,0:T(8,128)(2,1)S(1)}, u32[]{:S(2)}, u32[]{:S(2)}) async-start(bf16[128,72,128]{2,1,0:T(8,128)(2,1)} %send_1.1), calls=%async_computation | async-start | bytes 4718592 | tf_op jit(solution)/shard_map/all_to_all | solution.py:323
  48.1 31.2 %copy-start.8 = (s32[24576]{0:T(1024)}, s32[24576]{0:T(1024)S(1)}, u32[]{:S(2)}) copy-start(s32[24576]{0:T(1024)S(1)} %get-tuple-element.110) | copy-start | bytes 294916
  79.3 1.4 copy-start.3
  110.8 23.7 %copy-start.16 = (bf16[256,40]{0,1:T(8,128)(2,1)S(1)}, bf16[256,40]{0,1:T(8,128)(2,1)}, u32[]{:S(2)}) copy-start(bf16[256,40]{0,1:T(8,128)(2,1)} %param.30) | copy-start | bytes 61444
  110.8 23.8 %copy-start.17 = (bf16[256,40]{0,1:T(8,128)(2,1)S(1)}, bf16[256,40]{0,1:T(8,128)(2,1)}, u32[]{:S(2)}) copy-start(bf16[256,40]{0,1:T(8,128)(2,1)} %param.29) | copy-start | bytes 61444
  110.8 27.2 %copy-start.24 = (f32[40]{0:T(128)S(1)}, f32[40]{0:T(128)}, u32[]{:S(2)}) copy-start(f32[40]{0:T(128)} %param.31) | copy-start | bytes 484
  122.4 45.5 %all-to-all-start.1 = ((bf16[128,64,128]{2,1,0:T(8,128)(2,1)}), bf16[128,64,128]{2,1,0:T(8,128)(2,1)S(1)}, u32[]{:S(2)}, u32[]{:S(2)}) async-start(bf16[128,64,128]{2,1,0:T(8,128)(2,1)} %send_2.1), calls=%async_computation.1 | async-start | bytes 4194304 | tf_op jit(solution)/shard_map/all_to_all | solution.py:323
  134.2 31.5 %copy-start.12 = (s32[8192]{0:T(1024)}, s32[8192]{0:T(1024)S(1)}, u32[]{:S(2)}) copy-start(s32[8192]{0:T(1024)S(1)} %get-tuple-element.113) | copy-start | bytes 98308
  167.8 1.3 copy-start.4
  206.6 21.1 %copy-start.13 = (f32[12288]{0:T(1024)S(1)}, f32[12288]{0:T(1024)}, u32[]{:S(2)}) copy-start(f32[12288]{0:T(1024)} %param.18) | copy-start | bytes 147460
  206.6 21.1 %copy-start.19 = (s32[12288]{0:T(1024)S(1)}, s32[12288]{0:T(1024)}, u32[]{:S(2)}) copy-start(s32[12288]{0:T(1024)} %param.17) | copy-start | bytes 147460
  218.2 42.5 %all-to-all-start.2 = ((bf16[128,64,128]{2,1,0:T(8,128)(2,1)}), bf16[128,64,128]{2,1,0:T(8,128)(2,1)S(1)}, u32[]{:S(2)}, u32[]{:S(2)}) async-start(bf16[128,64,128]{2,1,0:T(8,128)(2,1)} %send_3.1), calls=%async_computation.2 | async-start | bytes 4194304 | tf_op jit(solution)/shard_map/all_to_all | solution.py:323
  260.7 1.3 copy-start.6
  296.0 34.0 %copy-start.10 = (bf16[256,256]{1,0:T(8,128)(2,1)S(1)}, bf16[256,256]{1,0:T(8,128)(2,1)}, u32[]{:S(2)}) copy-start(bf16[256,256]{1,0:T(8,128)(2,1)} %refs_6_.1) | copy-start | bytes 393220
  317.9 46.3 %all-to-all-start.3 = ((bf16[128,64,128]{2,1,0:T(8,128)(2,1)}), bf16[128,64,128]{2,1,0:T(8,128)(2,1)S(1)}, u32[]{:S(2)}, u32[]{:S(2)}) async-start(bf16[128,64,128]{2,1,0:T(8,128)(2,1)} %bitcast.61), calls=%async_computation.3 | async-start | bytes 4194304 | tf_op jit(solution)/shard_map/all_to_all | solution.py:323
  364.2 1.3 copy-start.5
  418.0 6.9 %copy-start.11 = (bf16[256,256]{1,0:T(8,128)(2,1)S(1)}, bf16[256,256]{1,0:T(8,128)(2,1)}, u32[]{:S(2)}) copy-start(bf16[256,256]{1,0:T(8,128)(2,1)} %refs_5_.3) | copy-start | bytes 393220
  418.0 7.7 %copy-start.7 = (bf16[12288,128]{1,0:T(8,128)(2,1)S(1)}, bf16[12288,128]{1,0:T(8,128)(2,1)}, u32[]{:S(2)}) copy-start(bf16[12288,128]{1,0:T(8,128)(2,1)} %get-tuple-element.31.refs_2_) | copy-start | bytes 9437188
  418.0 65.5 %all-to-all-start.4 = ((bf16[128,64,256]{2,1,0:T(8,128)(2,1)}), bf16[128,64,256]{2,1,0:T(8,128)(2,1)}, u32[]{:S(2)}, u32[]{:S(2)}) async-start(bf16[128,64,256]{2,1,0:T(8,128)(2,1)} %bitcast.59), calls=%async_computation.4 | async-start | bytes 8388608 | tf_op jit(solution)/shard_map/all_to_all | solution.py:323
  424.9 5.5 copy-start.23
  424.9 6.1 %copy-start.22 = (f32[8,128]{1,0:T(8,128)S(1)}, f32[8,128]{1,0:T(8,128)}, u32[]{:S(2)}) copy-start(f32[8,128]{1,0:T(8,128)} %get-tuple-element.40) | copy-start | bytes 12292
  431.1 12.6 %slice-start = ((s8[6291456]{0:T(1024)(128)(4,1)}), s8[2097152]{0:T(1024)(128)(4,1)S(1)}, s32[]{:S(2)}) async-start(s8[6291456]{0:T(1024)(128)(4,1)} %bitcast.57), calls=%async_computation.7 | async-start | bytes 4194304
  436.9 6.7 %slice-start.1 = ((s8[6291456]{0:T(1024)(128)(4,1)}), s8[4194304]{0:T(1024)(128)(4,1)S(1)}, s32[]{:S(2)}) async-start(s8[6291456]{0:T(1024)(128)(4,1)} %bitcast.57), calls=%async_computation.8 | async-start | bytes 8388608
  443.7 4.8 copy-start.20
  483.5 27.6 %copy-start.2 = (bf16[12288,128]{1,0:T(8,128)(2,1)S(1)}, bf16[12288,128]{1,0:T(8,128)(2,1)}, u32[]{:S(2)}) copy-start(bf16[12288,128]{1,0:T(8,128)(2,1)} %get-tuple-element.26.src_ref) | copy-start | bytes 9437188
  511.1 4.6 copy-start
  511.1 5.5 copy-start.1
  516.6 2.2 copy-start.21
